TPU v7x, 32 devices: a whole 2x2x4 slice. The times are simulated.
32 devices in a mesh: dp: 8 (over z, x), entry: 4 (over y, core).
Axes of the slice: x: 2, y: 2, z: 4, core: 2. Of those that a mesh axis runs over, the one named last changes fastest.
Arguments:
- frames: float32 [2048, 1024], P('dp'), may hold values from -100 to 100, as said below
- depth: int32 [8], P('dp'), may hold values from 1 to 2
- code_one: float32 [8192, 1024], P(('entry', 'dp')), may hold values from -0.5 to 0.5, as said below
- code_two: float32 [8192, 1024], P(('entry', 'dp')), may hold values from -0.5 to 0.5, as said below
Outputs:
- new_one: float32 [8192, 1024], P(('entry', 'dp'))
- new_two: float32 [8192, 1024], P(('entry', 'dp'))
Inputs may be any that keep to these rules, and one draw needn't show every extreme that they name: `frames`: Real-valued embeddings. `code_one`: Real-valued entries. `code_two`: Real-valued entries.
All inputs are finite; a program needn't handle non-finite values.
Results may differ from a plain program's by a relative error of at most 0.012.
Values may be sent and summed in bfloat16 or wider, within the bound.
No kernel may reach another device: no remote copies, remote signals or barrier semaphores. Data moves between devices by JAX's collectives and lax.ppermute only.
A program may use at most 128 MiB of HBM per device.

v0:
```python
import functools
import math

import jax
import jax.numpy as jnp
from jax import lax
from jax.experimental import pallas as pl
from jax.experimental.pallas import tpu as pltpu
from jax.sharding import PartitionSpec as P


EXTRA = 128
BYTES = 28 * 1024 * 1024
FAR = 3.0e38
NT = (((1,), (1,)), ((), ()))
NN = (((1,), (0,)), ((), ()))
BF = jnp.bfloat16
F32 = jnp.float32


def as_row(column):
    return jnp.broadcast_to(column, (column.shape[0], EXTRA)).T[0:1, :]


def half_column(book):
    wide = book.astype(F32)
    return 0.5 * jnp.sum(wide * wide, axis=1, keepdims=True)


def split(value):
    high = value.astype(BF).astype(F32)
    rest = value - high
    middle = rest.astype(BF).astype(F32)
    return high, middle, rest - middle


def attend_kernel(n_rows, n_books, rebuild, *refs):
    row_refs, book_refs = refs[:n_rows], refs[n_rows : n_rows + n_books]
    outs, (rows, score) = refs[n_rows + n_books : -2], refs[-2:]
    part = row_refs[0].shape[0]
    for j in range(n_rows):
        rows[j * part : (j + 1) * part, :] = row_refs[j][...]
    peak = None
    for j in range(n_books):
        book = book_refs[j][...]
        s = lax.dot_general(rows[...], book, NT, preferred_element_type=F32)
        s = s - as_row(half_column(book))
        score[j, :, : s.shape[1]] = s
        top = jnp.max(s, axis=1, keepdims=True)
        peak = top if peak is None else jnp.maximum(peak, top)
    total = None
    rebuilt = None
    for j in range(n_books):
        expo = jnp.exp(score[j, :, : book_refs[j].shape[0]] - peak)
        mass = jnp.sum(expo, axis=1, keepdims=True)
        total = mass if total is None else total + mass
        if rebuild:
            term = lax.dot_general(expo.astype(BF), book_refs[j][...], NN, preferred_element_type=F32)
            rebuilt = term if rebuilt is None else rebuilt + term
    level = peak + jnp.log(total)
    if not rebuild:
        weight_ref, out_ref = outs
        frames = level.shape[0]
        out_ref[:, :frames] = as_row(level)
        out_ref[:, frames:] = weight_ref[...]
        return
    width = rebuilt.shape[1]
    rebuilt = rebuilt / total
    parts = split(level)
    lane = lax.broadcasted_iota(jnp.int32, (part, EXTRA), 1)
    for j in range(n_rows):
        here = slice(j * part, (j + 1) * part)
        outs[j][:, :width] = rebuilt[here].astype(BF)
        tail = jnp.zeros((part, EXTRA), F32)
        for t in range(n_rows):
            m = (j + t) % n_rows
            for n, value in enumerate(parts):
                tail = jnp.where(lane == 3 * t + n, value[m * part : (m + 1) * part], tail)
        outs[j][:, width:] = tail.astype(BF)


def attend(rows, books, part, weight=None):
    rebuild = weight is None
    more = () if rebuild else (weight,)
    width = books[0].shape[1]
    entries = books[0].shape[0]
    frames = part * len(rows)
    if rebuild:
        out_shape = [jax.ShapeDtypeStruct((part, width + EXTRA), BF)] * len(rows)
    else:
        out_shape = [jax.ShapeDtypeStruct((1, frames + part), F32)]
    total = sum(book.shape[0] for book in books)
    work = 2 * frames * total * width
    return pl.pallas_call(
        functools.partial(attend_kernel, len(rows), len(books), rebuild),
        grid=(1,),
        out_shape=out_shape,
        in_specs=[pl.BlockSpec((part, width), lambda i: (0, 0))] * len(rows)
        + [pl.BlockSpec(book.shape, lambda i: (0, 0)) for book in books + list(more)],
        out_specs=[pl.BlockSpec(s.shape, lambda i: (0, 0)) for s in out_shape],
        scratch_shapes=[
            pltpu.VMEM((frames, width), BF),
            pltpu.VMEM((len(books), frames, entries), F32),
        ],
        compiler_params=pltpu.CompilerParams(vmem_limit_bytes=BYTES),
        cost_estimate=pl.CostEstimate(
            flops=work * (2 if rebuild else 1),
            bytes_accessed=2 * width * (frames + total),
            transcendentals=frames * total,
        ),
        name="attend" if rebuild else "levels",
    )(*rows, *books, *more)


def merge_levels(parts):
    top = functools.reduce(jnp.maximum, parts)
    return top + jnp.log(sum(jnp.exp(part - top) for part in parts))


def combine_kernel(n, *refs):
    frame_ref, piece_refs, (second_ref, level_ref) = refs[0], refs[1 : 1 + n], refs[1 + n :]
    part, width = frame_ref.shape
    tails = [ref[:, width:].astype(F32) for ref in piece_refs]
    for t in reversed(range(n)):
        parts = [tail[:, 3 * t : 3 * t + 1] + tail[:, 3 * t + 1 : 3 * t + 2] + tail[:, 3 * t + 2 : 3 * t + 3] for tail in tails]
        level = merge_levels(parts)
        level_ref[:, t * part : (t + 1) * part] = as_row(level)
    rebuilt = None
    for ref, p in zip(piece_refs, parts):
        term = jnp.exp(p - level) * ref[:, :width].astype(F32)
        rebuilt = term if rebuilt is None else rebuilt + term
    second_ref[...] = (frame_ref[...] - rebuilt).astype(BF)


def combine(frames, pieces):
    part, width = frames.shape
    n = len(pieces)
    return pl.pallas_call(
        functools.partial(combine_kernel, n),
        out_shape=[jax.ShapeDtypeStruct((part, width), BF), jax.ShapeDtypeStruct((1, n * part), F32)],
        in_specs=[pl.BlockSpec(memory_space=pltpu.VMEM)] * (1 + n),
        out_specs=[pl.BlockSpec(memory_space=pltpu.VMEM)] * 2,
        compiler_params=pltpu.CompilerParams(vmem_limit_bytes=BYTES // 4),
        cost_estimate=pl.CostEstimate(flops=4 * part * width * n, bytes_accessed=4 * part * width * n, transcendentals=0),
        name="combine",
    )(frames, *pieces)


def stats_kernel(part, *refs):
    note_refs, out_ref = refs[:-1], refs[-1]
    many = part * len(note_refs)
    turned = []
    for j, ref in enumerate(note_refs):
        row = jnp.broadcast_to(ref[:, :many], (8, many))
        turned.append(pltpu.roll(row, j * part, 1) if j else row)
        out_ref[:, j * part : (j + 1) * part] = ref[:, many:]
    level = merge_levels(turned)[0:1]
    out_ref[...] = jnp.where(out_ref[...] > 0.0, level, FAR)


def stats_of(notes, part):
    return pl.pallas_call(
        functools.partial(stats_kernel, part),
        out_shape=jax.ShapeDtypeStruct((1, part * len(notes)), F32),
        in_specs=[pl.BlockSpec(memory_space=pltpu.VMEM)] * len(notes),
        out_specs=pl.BlockSpec(memory_space=pltpu.VMEM),
        compiler_params=pltpu.CompilerParams(vmem_limit_bytes=BYTES // 8),
        cost_estimate=pl.CostEstimate(flops=100000, bytes_accessed=20000, transcendentals=2000),
        name="stats",
    )(*notes)


def sums_kernel(counts, n_before, refreshed, *refs):
    n_chunks, n_pieces = len(counts), sum(counts)
    piece_refs, rest = refs[:n_pieces], refs[n_pieces:]
    stat_refs, rest = rest[:n_chunks], rest[n_chunks:]
    book_ref, before, rest = rest[0], rest[1 : 1 + n_before], rest[1 + n_before :]
    out_ref, hold = rest[-2:]
    book = book_ref[...]
    width = book.shape[1]
    half = half_column(book)
    num = None
    den = None
    at = 0
    for j, count in enumerate(counts):
        if count == 1:
            chunk = piece_refs[at][...]
        else:
            row_at = 0
            for ref in piece_refs[at : at + count]:
                hold[j % 2, row_at : row_at + ref.shape[0], :] = ref[...]
                row_at += ref.shape[0]
            chunk = hold[j % 2]
        at += count
        s = lax.dot_general(book, chunk, NT, preferred_element_type=F32) - half
        prob = jnp.exp(s - stat_refs[j][...])
        mass = jnp.sum(prob, axis=1, keepdims=True)
        term = lax.dot_general(prob.astype(BF), chunk, NN, preferred_element_type=F32)
        num = term if num is None else num + term
        den = mass if den is None else den + mass
    for ref in before:
        num = num + ref[:, :width]
        den = den + ref[:, width : width + 1]
    if refreshed:
        out_ref[...] = (num + rest[0][...]) / (den + 1.0)
    else:
        out_ref[:, :width] = num
        out_ref[:, width:] = jnp.broadcast_to(den, (den.shape[0], EXTRA))


def sums(chunks, stats, book, before=(), code=None):
    entries, width = book.shape
    pieces = [piece for chunk in chunks for piece in chunk]
    frames = sum(piece.shape[0] for piece in pieces)
    codes = () if code is None else (code,)
    ins = (*pieces, *stats, book, *before, *codes)
    return pl.pallas_call(
        functools.partial(sums_kernel, tuple(len(chunk) for chunk in chunks), len(before), bool(codes)),
        out_shape=jax.ShapeDtypeStruct((entries, width + (0 if codes else EXTRA)), F32),
        in_specs=[pl.BlockSpec(memory_space=pltpu.VMEM)] * len(ins),
        out_specs=pl.BlockSpec(memory_space=pltpu.VMEM),
        scratch_shapes=[pltpu.VMEM((2, stats[0].shape[1], width), BF)],
        compiler_params=pltpu.CompilerParams(vmem_limit_bytes=BYTES),
        cost_estimate=pl.CostEstimate(
            flops=4 * frames * entries * width,
            bytes_accessed=2 * width * frames + 6 * width * entries,
            transcendentals=frames * entries,
        ),
        name="sums",
    )(*ins)


def build(lz, lx, ly, lc):
    entry = ly * lc
    axes = ("dp", "entry")
    sizes = (lz, lx, ly, lc)

    def shift(value, z=0, x=0, y=0, c=0):
        pairs = []
        for source in range(lz * lx * entry):
            rest, place = source, []
            for size in reversed(sizes):
                rest, digit = divmod(rest, size)
                place.append(digit)
            to = 0
            for digit, size, step in zip(reversed(place), sizes, (z, x, y, c)):
                to = to * size + (digit + step) % size
            pairs.append((source, to))
        return lax.ppermute(value, axes, pairs)

    far = [(i, k) for i in range(lx) for k in range(ly)][1:]

    def spread(value):
        return [shift(value, x=i, y=k) for i, k in far]

    straight = [(i, k) for i, k in far if i == 0 or k == 0]
    bent = [(i, k) for i, k in far if i and k]

    def layer(book):
        near = [shift(book, c=m) for m in range(1, lc)]
        got = {(i, k): shift(book, x=i, y=k) for i, k in straight}
        cut = book.shape[0] // 2
        handed = []
        for i, k in bent:
            handed.append(shift(got[0, k][:cut], x=i))
            handed.append(shift(got[i, 0][cut:], y=k))
        pieces = list(got.values())
        across = [shift(p, c=m) for p in pieces for m in range(1, lc)]
        around = [shift(p, c=m) for p in handed for m in range(1, lc)]
        return [book] + near, pieces + handed + across + around

    def on_device(frames, depth, code_one, code_two):
        place = lax.axis_index("entry")
        y, c = place // lc, place % lc
        part = frames.shape[0] // entry
        book_one = code_one.astype(BF)
        book_two = code_two.astype(BF)
        near_one, far_one = layer(book_one)
        starts = [(c * ly + (y - k) % ly) * part for k in range(ly)]
        rows = [lax.dynamic_slice_in_dim(frames, s, part, 0) for s in starts]
        own = rows[0].astype(BF)
        slabs = [own] + [shift(own, z=j) for j in range(1, lz)]
        other = jnp.concatenate(rows[1:], 0).astype(BF) if ly > 1 else own[:0]
        others = [other] + [shift(other, z=j) for j in range(1, lz)] if ly > 1 else []
        pieces = attend(slabs, near_one + far_one, part)
        returned = [pieces[0]] + [shift(pieces[j], z=-j) for j in range(1, lz)]
        near_two, far_two = layer(book_two)

        first = jnp.concatenate(slabs, 0)
        cut = first.shape[0] // 2
        mine = [[piece[(k - 1) * part : k * part] for piece in others] for k in range(1, ly)]
        halves = [jnp.concatenate(m[: len(m) // 2], 0) for m in mine]
        chunks_one = [[first]] + [list(m) for m in mine]
        for i in range(1, lx):
            moved = shift(first, x=i)
            chunks_one.append([moved])
            for k in range(1, ly):
                chunks_one.append([shift(halves[k - 1], x=i), shift(moved[cut:], y=k)])

        group = frames.shape[0] // depth.shape[0]
        if depth.shape[0] == 1:
            weight = jnp.broadcast_to((depth == 2).astype(F32)[:, None], (1, part))
        else:
            weight = jnp.repeat((depth == 2).astype(F32), group)
            weight = lax.dynamic_slice_in_dim(weight, starts[0], part, 0).reshape(1, part)
        second, level = combine(rows[0], returned)

        seconds = [second] + [shift(second, z=j) for j in range(1, lz)]
        ahead = spread(second)
        stats = [level] + spread(level)
        rest = spread(jnp.concatenate(seconds[1:], 0))
        chunks_two = [seconds] + [list(chunk) for chunk in zip(ahead, rest)]
        (note,) = attend(seconds, near_two + far_two, part, weight)
        notes = [note] + [shift(note, z=j) for j in range(1, lz)]

        others = [sums(chunks_one, stats, near_one[m]) for m in range(1, lc)]
        sent = [shift(other, c=-m) for m, other in enumerate(others, 1)]
        new_one = sums(chunks_one, stats, near_one[0], sent, code_one)

        stats = stats_of(notes, part)
        stats = [stats] + spread(stats)
        early = [sums(chunks_two[:-1], stats[:-1], near_two[m]) for m in range(lc)]
        sent = [shift(other, c=-m) for m, other in enumerate(early[1:], 1)]
        last = [chunks_two[-1][0], chunks_two[-1][1]]
        last = [last] + [[shift(last[0], c=m), shift(last[1], c=m)] for m in range(1, lc)]
        stats = [stats[-1]] + [shift(stats[-1], c=m) for m in range(1, lc)]
        new_two = sums(last, stats, near_two[0], [early[0]] + sent, code_two)
        return new_one, new_two

    return on_device


def solution(mesh):
    dp, entry = mesh.shape["dp"], mesh.shape["entry"]
    lz = math.gcd(dp, entry)
    lc = 2 if entry % 2 == 0 else 1
    lx, ly = dp // lz, entry // lc
    return jax.shard_map(
        build(lz, lx, ly, lc),
        mesh=mesh,
        in_specs=(P("dp", None), P("dp"), P(("entry", "dp"), None), P(("entry", "dp"), None)),
        out_specs=(P(("entry", "dp"), None), P(("entry", "dp"), None)),
        check_vma=False,
    )
```

profile of v0, /device:TPU:0, one launch (start us, length us, event | category | flops | bytes accessed | tf_op | source)
XLA Modules:
  0.0 160.5 jit_solution(6485112418877062735)
XLA Ops:
  1.9 3.1 %collective-permute-start.10 = (bf16[256,1024]{1,0:T(8,128)(2,1)S(1)}, bf16[256,1024]{1,0:T(8,128)(2,1)}, u32[]{:S(2)}, u32[]{:S(2)}) collective-permute-start(bf16[256,1024]{1,0:T(8,128)(2,1)S(1)} %convert_element_type.15.refs_4_.refs_12_), channel_id=1, source_target_pairs={{0,2},{1,3},{2,0},{3,1},{4,6},{5,7},{6,4},{7,5},{8,10},{9,11},{10,... | collective-permute-start | bytes 1572872 | tf_op jit(solution)/shard_map/ppermute | solution.py:249
  6.5 10.5 %collective-permute-done.10.refs_6_ = bf16[256,1024]{1,0:T(8,128)(2,1)} collective-permute-done((bf16[256,1024]{1,0:T(8,128)(2,1)S(1)}, bf16[256,1024]{1,0:T(8,128)(2,1)}, u32[]{:S(2)}, u32[]{:S(2)}) %collective-permute-start.10) | collective-permute-done | bytes 524320 | tf_op jit(solution)/shard_map/ppermute | solution.py:249
  18.0 1.8 %collective-permute-start.12 = (bf16[128,1024]{1,0:T(8,128)(2,1)S(1)}, bf16[128,1024]{1,0:T(8,128)(2,1)S(1)}, u32[]{:S(2)}, u32[]{:S(2)}) collective-permute-start(bf16[128,1024]{1,0:T(8,128)(2,1)S(1)} %slice.21), channel_id=1, source_target_pairs={{0,4},{1,5},{2,6},{3,7},{4,0},{5,1},{6,2},{7,3},{8,12},{9,13},{10,... | collective-permute-start | bytes 786440 | tf_op jit(solution)/shard_map/ppermute | solution.py:249
  20.8 1.6 %collective-permute-start = (bf16[64,1024]{1,0:T(8,128)(2,1)S(1)}, bf16[64,1024]{1,0:T(8,128)(2,1)S(1)}, u32[]{:S(2)}, u32[]{:S(2)}) collective-permute-start(bf16[64,1024]{1,0:T(8,128)(2,1)S(1)} %get-tuple-element.14.refs_0_), channel_id=1, source_target_pairs={{0,8},{1,9},{2,10},{3,11},{4,12},{5,13},{6,14},{7,15},{8,16},{9,17... | collective-permute-start | bytes 393224 | tf_op jit(solution)/shard_map/ppermute | solution.py:249
  22.4 2.6 %collective-permute-start.1 = (bf16[64,1024]{1,0:T(8,128)(2,1)S(1)}, bf16[64,1024]{1,0:T(8,128)(2,1)S(1)}, u32[]{:S(2)}, u32[]{:S(2)}) collective-permute-start(bf16[64,1024]{1,0:T(8,128)(2,1)S(1)} %get-tuple-element.14.refs_0_), channel_id=1, source_target_pairs={{0,16},{1,17},{2,18},{3,19},{4,20},{5,21},{6,22},{7,23},{8,24},{9,... | collective-permute-start | bytes 393224 | tf_op jit(solution)/shard_map/ppermute | solution.py:249
  27.3 1.7 %collective-permute-done.refs_1_ = bf16[64,1024]{1,0:T(8,128)(2,1)S(1)} collective-permute-done((bf16[64,1024]{1,0:T(8,128)(2,1)S(1)}, bf16[64,1024]{1,0:T(8,128)(2,1)S(1)}, u32[]{:S(2)}, u32[]{:S(2)}) %collective-permute-start) | collective-permute-done | bytes 131104 | tf_op jit(solution)/shard_map/ppermute | solution.py:249
  30.6 2.0 %collective-permute-done.1.refs_2_ = bf16[64,1024]{1,0:T(8,128)(2,1)S(1)} collective-permute-done((bf16[64,1024]{1,0:T(8,128)(2,1)S(1)}, bf16[64,1024]{1,0:T(8,128)(2,1)S(1)}, u32[]{:S(2)}, u32[]{:S(2)}) %collective-permute-start.1) | collective-permute-done | bytes 131104 | tf_op jit(solution)/shard_map/ppermute | solution.py:249
  33.2 2.3 %collective-permute-done.13.refs_9_ = bf16[128,1024]{1,0:T(8,128)(2,1)} collective-permute-done((bf16[128,1024]{1,0:T(8,128)(2,1)S(1)}, bf16[128,1024]{1,0:T(8,128)(2,1)}, u32[]{:S(2)}, u32[]{:S(2)}) %collective-permute-start.13) | collective-permute-done | bytes 262176 | tf_op jit(solution)/shard_map/ppermute | solution.py:249
  40.2 3.6 %collective-permute-start.3 = (bf16[64,1024]{1,0:T(8,128)(2,1)S(1)}, bf16[64,1024]{1,0:T(8,128)(2,1)S(1)}, u32[]{:S(2)}, u32[]{:S(2)}) collective-permute-start(bf16[64,1024]{1,0:T(8,128)(2,1)S(1)} %dynamic-slice_convert_fusion.refs_1_), channel_id=1, source_target_pairs={{0,8},{1,9},{2,10},{3,11},{4,12},{5,13},{6,14},{7,15},{8,16},{9,17... | collective-permute-start | bytes 393224 | tf_op jit(solution)/shard_map/ppermute | solution.py:249
  43.9 2.0 %collective-permute-start.4 = (bf16[64,1024]{1,0:T(8,128)(2,1)S(1)}, bf16[64,1024]{1,0:T(8,128)(2,1)S(1)}, u32[]{:S(2)}, u32[]{:S(2)}) collective-permute-start(bf16[64,1024]{1,0:T(8,128)(2,1)S(1)} %dynamic-slice_convert_fusion.refs_1_), channel_id=1, source_target_pairs={{0,16},{1,17},{2,18},{3,19},{4,20},{5,21},{6,22},{7,23},{8,24},{9,... | collective-permute-start | bytes 393224 | tf_op jit(solution)/shard_map/ppermute | solution.py:249
  45.9 2.8 %collective-permute-start.5 = (bf16[64,1024]{1,0:T(8,128)(2,1)S(1)}, bf16[64,1024]{1,0:T(8,128)(2,1)S(1)}, u32[]{:S(2)}, u32[]{:S(2)}) collective-permute-start(bf16[64,1024]{1,0:T(8,128)(2,1)S(1)} %dynamic-slice_convert_fusion.refs_1_), channel_id=1, source_target_pairs={{0,24},{1,25},{2,26},{3,27},{4,28},{5,29},{6,30},{7,31},{8,0},{9,1... | collective-permute-start | bytes 393224 | tf_op jit(solution)/shard_map/ppermute | solution.py:249
  54.4 5.3 %attend.1 = (bf16[64,1152]{1,0:T(8,128)(2,1)S(1)}, bf16[64,1152]{1,0:T(8,128)(2,1)S(1)}, bf16[64,1152]{1,0:T(8,128)(2,1)S(1)}, bf16[64,1152]{1,0:T(8,128)(2,1)S(1)}) custom-call(bf16[64,1024]{1,0:T(8,128)(2,1)S(1)} %get-tuple-element.14.refs_0_, bf16[64,1024]{1,0:T(8,128)(2,1)S(1)} %copy-done.3, bf16[64,1024]{1,0:T(8,128)(2,1)S(1)} %copy-done.6, ...), custom_call_target="tpu_custom_call" | custom-call | flops 2147483648 | bytes 4718592 | tf_op jit(solution)/shard_map/attend/pallas_call | solution.py:94
  60.5 1.6 collective-permute-start.6
  63.6 3.7 %collective-permute-done.18.refs_2_ = bf16[64,1152]{1,0:T(8,128)(2,1)S(1)} collective-permute-done((bf16[64,1152]{1,0:T(8,128)(2,1)S(1)}, bf16[64,1152]{1,0:T(8,128)(2,1)S(1)}, u32[]{:S(2)}, u32[]{:S(2)}) %collective-permute-start.18) | collective-permute-done | bytes 147488 | tf_op jit(solution)/shard_map/ppermute | solution.py:249
  68.3 6.3 %collective-permute-done.19.refs_3_ = bf16[64,1152]{1,0:T(8,128)(2,1)S(1)} collective-permute-done((bf16[64,1152]{1,0:T(8,128)(2,1)S(1)}, bf16[64,1152]{1,0:T(8,128)(2,1)S(1)}, u32[]{:S(2)}, u32[]{:S(2)}) %collective-permute-start.19) | collective-permute-done | bytes 147488 | tf_op jit(solution)/shard_map/ppermute | solution.py:249
  76.6 4.3 %collective-permute-done.7.refs_6_ = bf16[128,1024]{1,0:T(8,128)(2,1)S(1)} collective-permute-done((bf16[128,1024]{1,0:T(8,128)(2,1)S(1)}, bf16[128,1024]{1,0:T(8,128)(2,1)S(1)}, u32[]{:S(2)}, u32[]{:S(2)}) %collective-permute-start.7) | collective-permute-done | bytes 262176 | tf_op jit(solution)/shard_map/ppermute | solution.py:249
  82.5 3.0 %collective-permute-done.35.refs_8_ = bf16[128,1024]{1,0:T(8,128)(2,1)S(1)} collective-permute-done((bf16[128,1024]{1,0:T(8,128)(2,1)S(1)}, bf16[128,1024]{1,0:T(8,128)(2,1)S(1)}, u32[]{:S(2)}, u32[]{:S(2)}) %collective-permute-start.35) | collective-permute-done | bytes 262176 | tf_op jit(solution)/shard_map/ppermute | solution.py:249
  86.1 1.7 %collective-permute-done.26.refs_1_ = bf16[64,1024]{1,0:T(8,128)(2,1)S(1)} collective-permute-done((bf16[64,1024]{1,0:T(8,128)(2,1)S(1)}, bf16[64,1024]{1,0:T(8,128)(2,1)S(1)}, u32[]{:S(2)}, u32[]{:S(2)}) %collective-permute-start.26) | collective-permute-done | bytes 131104 | tf_op jit(solution)/shard_map/ppermute | solution.py:249
  87.7 3.9 %collective-permute-done.27.refs_2_ = bf16[64,1024]{1,0:T(8,128)(2,1)S(1)} collective-permute-done((bf16[64,1024]{1,0:T(8,128)(2,1)S(1)}, bf16[64,1024]{1,0:T(8,128)(2,1)S(1)}, u32[]{:S(2)}, u32[]{:S(2)}) %collective-permute-start.27) | collective-permute-done | bytes 131104 | tf_op jit(solution)/shard_map/ppermute | solution.py:249
  92.9 3.9 %collective-permute-done.28.refs_3_ = bf16[64,1024]{1,0:T(8,128)(2,1)S(1)} collective-permute-done((bf16[64,1024]{1,0:T(8,128)(2,1)S(1)}, bf16[64,1024]{1,0:T(8,128)(2,1)S(1)}, u32[]{:S(2)}, u32[]{:S(2)}) %collective-permute-start.28) | collective-permute-done | bytes 131104 | tf_op jit(solution)/shard_map/ppermute | solution.py:249
  99.0 1.5 collective-permute-start.21
  102.7 6.3 %collective-permute-done.21.refs_9_ = f32[1,256]{1,0:T(1,128)S(1)} collective-permute-done((f32[1,256]{1,0:T(1,128)S(1)}, f32[1,256]{1,0:T(1,128)S(1)}, u32[]{:S(2)}, u32[]{:S(2)}) %collective-permute-start.21) | collective-permute-done | bytes 1056 | tf_op jit(solution)/shard_map/ppermute | solution.py:249
  111.3 2.3 %levels.1.refs_0_ = f32[1,320]{1,0:T(1,128)S(1)} custom-call(bf16[64,1024]{1,0:T(8,128)(2,1)S(1)} %get-tuple-element.13.refs_0_, bf16[64,1024]{1,0:T(8,128)(2,1)S(1)} %collective-permute-done.26.refs_1_, bf16[64,1024]{1,0:T(8,128)(2,1)S(1)} %collective-permute-done.27.refs_2_, bf16[64,1024]{1,0:T(8,128)(2,1)S(1)} %collective-permute-done.28.refs_3_, ...), custom_call_target="tpu_custom_call" | custom-call | flops 1073741824 | bytes 4718592 | tf_op jit(solution)/shard_map/levels/pallas_call | solution.py:94
  115.0 5.4 %collective-permute-done.41.refs_1_ = f32[1,320]{1,0:T(1,128)S(1)} collective-permute-done((f32[1,320]{1,0:T(1,128)S(1)}, f32[1,320]{1,0:T(1,128)S(1)}, u32[]{:S(2)}, u32[]{:S(2)}) %collective-permute-start.41) | collective-permute-done | bytes 1312 | tf_op jit(solution)/shard_map/ppermute | solution.py:249
  120.4 4.5 %collective-permute-done.42.refs_2_ = f32[1,320]{1,0:T(1,128)S(1)} collective-permute-done((f32[1,320]{1,0:T(1,128)S(1)}, f32[1,320]{1,0:T(1,128)S(1)}, u32[]{:S(2)}, u32[]{:S(2)}) %collective-permute-start.42) | collective-permute-done | bytes 1312 | tf_op jit(solution)/shard_map/ppermute | solution.py:249
  125.9 1.9 %sums.5 = f32[256,1152]{1,0:T(8,128)S(1)} custom-call(bf16[256,1024]{1,0:T(8,128)(2,1)S(1)} %pad_maximum_fusion.refs_0_, bf16[64,1024]{1,0:T(8,128)(2,1)S(1)} %dynamic-slice_convert_fusion.refs_1_, bf16[64,1024]{1,0:T(8,128)(2,1)S(1)} %collective-permute-done.3.refs_2_, bf16[64,1024]{1,0:T(8,128)(2,1)S(1)} %collective-permute-done.4.refs_3_, ...), custom_call_target="tpu_custom_call" | custom-call | flops 1073741824 | bytes 3670016 | tf_op jit(solution)/shard_map/sums/pallas_call | solution.py:217
  130.6 1.6 %collective-permute-done.50.refs_9_ = f32[1,256]{1,0:T(1,128)S(1)} collective-permute-done((f32[1,256]{1,0:T(1,128)S(1)}, f32[1,256]{1,0:T(1,128)S(1)}, u32[]{:S(2)}, u32[]{:S(2)}) %collective-permute-start.50) | collective-permute-done | bytes 1056 | tf_op jit(solution)/shard_map/ppermute | solution.py:249
  134.3 1.6 collective-permute-start.29
  135.9 10.9 %collective-permute-done.29.refs_1_ = bf16[192,1024]{1,0:T(8,128)(2,1)S(1)} collective-permute-done((bf16[192,1024]{1,0:T(8,128)(2,1)S(1)}, bf16[192,1024]{1,0:T(8,128)(2,1)S(1)}, u32[]{:S(2)}, u32[]{:S(2)}) %collective-permute-start.29) | collective-permute-done | bytes 393248 | tf_op jit(solution)/shard_map/ppermute | solution.py:249
  149.7 3.9 %collective-permute-done.25.refs_0_ = bf16[64,1024]{1,0:T(8,128)(2,1)S(1)} collective-permute-done((bf16[64,1024]{1,0:T(8,128)(2,1)S(1)}, bf16[64,1024]{1,0:T(8,128)(2,1)S(1)}, u32[]{:S(2)}, u32[]{:S(2)}) %collective-permute-start.25) | collective-permute-done | bytes 131104 | tf_op jit(solution)/shard_map/ppermute | solution.py:249
  155.6 2.9 %sums.6 = f32[256,1024]{1,0:T(8,128)} custom-call(bf16[256,1024]{1,0:T(8,128)(2,1)S(1)} %pad_maximum_fusion.refs_0_, bf16[64,1024]{1,0:T(8,128)(2,1)S(1)} %dynamic-slice_convert_fusion.refs_1_, bf16[64,1024]{1,0:T(8,128)(2,1)S(1)} %collective-permute-done.3.refs_2_, bf16[64,1024]{1,0:T(8,128)(2,1)S(1)} %collective-permute-done.4.refs_3_, ...), custom_call_target="tpu_custom_call" | custom-call | flops 1073741824 | bytes 3670016 | tf_op jit(solution)/shard_map/sums/pallas_call | solution.py:217
  158.5 1.9 %sums.9 = f32[256,1024]{1,0:T(8,128)} custom-call(bf16[64,1024]{1,0:T(8,128)(2,1)S(1)} %collective-permute-done.25.refs_0_, bf16[192,1024]{1,0:T(8,128)(2,1)S(1)} %collective-permute-done.29.refs_1_, bf16[64,1024]{1,0:T(8,128)(2,1)S(1)} %collective-permute-done.30.refs_2_, bf16[192,1024]{1,0:T(8,128)(2,1)S(1)} %collective-permute-done.31.refs_3_, ...), custom_call_target="tpu_custom_call" | custom-call | flops 536870912 | bytes 2621440 | tf_op jit(solution)/shard_map/sums/pallas_call | solution.py:217
  (132 shorter events, 46.3 us)
Async XLA Ops:
  1.9 15.1 %collective-permute-start.10 = (bf16[256,1024]{1,0:T(8,128)(2,1)S(1)}, bf16[256,1024]{1,0:T(8,128)(2,1)}, u32[]{:S(2)}, u32[]{:S(2)}) collective-permute-start(bf16[256,1024]{1,0:T(8,128)(2,1)S(1)} %convert_element_type.15.refs_4_.refs_12_), channel_id=1, source_target_pairs={{0,2},{1,3},{2,0},{3,1},{4,6},{5,7},{6,4},{7,5},{8,10},{9,11},{10,... | collective-permute-start | bytes 1572872 | tf_op jit(solution)/shard_map/ppermute | solution.py:249
  5.0 20.0 %collective-permute-start.11 = (bf16[256,1024]{1,0:T(8,128)(2,1)S(1)}, bf16[256,1024]{1,0:T(8,128)(2,1)}, u32[]{:S(2)}, u32[]{:S(2)}) collective-permute-start(bf16[256,1024]{1,0:T(8,128)(2,1)S(1)} %convert_element_type.15.refs_4_.refs_12_), channel_id=1, source_target_pairs={{0,4},{1,5},{2,6},{3,7},{4,0},{5,1},{6,2},{7,3},{8,12},{9,13},{10,... | collective-permute-start | bytes 1572872 | tf_op jit(solution)/shard_map/ppermute | solution.py:249
  6.5 29.1 %collective-permute-start.9 = (bf16[256,1024]{1,0:T(8,128)(2,1)S(1)}, bf16[256,1024]{1,0:T(8,128)(2,1)S(1)}, u32[]{:S(2)}, u32[]{:S(2)}) collective-permute-start(bf16[256,1024]{1,0:T(8,128)(2,1)S(1)} %convert_element_type.15.refs_4_.refs_12_), channel_id=1, source_target_pairs={{0,1},{1,0},{2,3},{3,2},{4,5},{5,4},{6,7},{7,6},{8,9},{9,8},{10,11... | collective-permute-start | bytes 1572872 | tf_op jit(solution)/shard_map/ppermute | solution.py:249
  18.0 15.1 %collective-permute-start.12 = (bf16[128,1024]{1,0:T(8,128)(2,1)S(1)}, bf16[128,1024]{1,0:T(8,128)(2,1)S(1)}, u32[]{:S(2)}, u32[]{:S(2)}) collective-permute-start(bf16[128,1024]{1,0:T(8,128)(2,1)S(1)} %slice.21), channel_id=1, source_target_pairs={{0,4},{1,5},{2,6},{3,7},{4,0},{5,1},{6,2},{7,3},{8,12},{9,13},{10,... | collective-permute-start | bytes 786440 | tf_op jit(solution)/shard_map/ppermute | solution.py:249
  22.4 10.2 %collective-permute-start.1 = (bf16[64,1024]{1,0:T(8,128)(2,1)S(1)}, bf16[64,1024]{1,0:T(8,128)(2,1)S(1)}, u32[]{:S(2)}, u32[]{:S(2)}) collective-permute-start(bf16[64,1024]{1,0:T(8,128)(2,1)S(1)} %get-tuple-element.14.refs_0_), channel_id=1, source_target_pairs={{0,16},{1,17},{2,18},{3,19},{4,20},{5,21},{6,22},{7,23},{8,24},{9,... | collective-permute-start | bytes 393224 | tf_op jit(solution)/shard_map/ppermute | solution.py:249
  32.6 11.3 %collective-permute-start.14 = (bf16[256,1024]{1,0:T(8,128)(2,1)}, bf16[256,1024]{1,0:T(8,128)(2,1)}, u32[]{:S(2)}, u32[]{:S(2)}) collective-permute-start(bf16[256,1024]{1,0:T(8,128)(2,1)} %collective-permute-done.10.refs_6_), channel_id=1, source_target_pairs={{0,1},{1,0},{2,3},{3,2},{4,5},{5,4},{6,7},{7,6},{8,9},{9,8},{10,11... | collective-permute-start | bytes 1572872 | tf_op jit(solution)/shard_map/ppermute | solution.py:249
  32.6 13.2 %collective-permute-start.15 = (bf16[256,1024]{1,0:T(8,128)(2,1)}, bf16[256,1024]{1,0:T(8,128)(2,1)}, u32[]{:S(2)}, u32[]{:S(2)}) collective-permute-start(bf16[256,1024]{1,0:T(8,128)(2,1)} %collective-permute-done.11.refs_7_), channel_id=1, source_target_pairs={{0,1},{1,0},{2,3},{3,2},{4,5},{5,4},{6,7},{7,6},{8,9},{9,8},{10,11... | collective-permute-start | bytes 1572872 | tf_op jit(solution)/shard_map/ppermute | solution.py:249
  36.5 25.6 %collective-permute-start.33 = (bf16[256,1024]{1,0:T(8,128)(2,1)S(1)}, bf16[256,1024]{1,0:T(8,128)(2,1)S(1)}, u32[]{:S(2)}, u32[]{:S(2)}) collective-permute-start(bf16[256,1024]{1,0:T(8,128)(2,1)S(1)} %convert_element_type.16.refs_4_.refs_11_.refs_6_), channel_id=1, source_target_pairs={{0,2},{1,3},{2,0},{3,1},{4,6},{5,7},{6,4},{7,5},{8,10},{9,11},{10,... | collective-permute-start | bytes 1572872 | tf_op jit(solution)/shard_map/ppermute | solution.py:249
  38.7 23.4 %collective-permute-start.34 = (bf16[256,1024]{1,0:T(8,128)(2,1)S(1)}, bf16[256,1024]{1,0:T(8,128)(2,1)S(1)}, u32[]{:S(2)}, u32[]{:S(2)}) collective-permute-start(bf16[256,1024]{1,0:T(8,128)(2,1)S(1)} %convert_element_type.16.refs_4_.refs_11_.refs_6_), channel_id=1, source_target_pairs={{0,4},{1,5},{2,6},{3,7},{4,0},{5,1},{6,2},{7,3},{8,12},{9,13},{10,... | collective-permute-start | bytes 1572872 | tf_op jit(solution)/shard_map/ppermute | solution.py:249
  40.2 19.5 %collective-permute-start.3 = (bf16[64,1024]{1,0:T(8,128)(2,1)S(1)}, bf16[64,1024]{1,0:T(8,128)(2,1)S(1)}, u32[]{:S(2)}, u32[]{:S(2)}) collective-permute-start(bf16[64,1024]{1,0:T(8,128)(2,1)S(1)} %dynamic-slice_convert_fusion.refs_1_), channel_id=1, source_target_pairs={{0,8},{1,9},{2,10},{3,11},{4,12},{5,13},{6,14},{7,15},{8,16},{9,17... | collective-permute-start | bytes 393224 | tf_op jit(solution)/shard_map/ppermute | solution.py:249
  43.9 15.9 %collective-permute-start.4 = (bf16[64,1024]{1,0:T(8,128)(2,1)S(1)}, bf16[64,1024]{1,0:T(8,128)(2,1)S(1)}, u32[]{:S(2)}, u32[]{:S(2)}) collective-permute-start(bf16[64,1024]{1,0:T(8,128)(2,1)S(1)} %dynamic-slice_convert_fusion.refs_1_), channel_id=1, source_target_pairs={{0,16},{1,17},{2,18},{3,19},{4,20},{5,21},{6,22},{7,23},{8,24},{9,... | collective-permute-start | bytes 393224 | tf_op jit(solution)/shard_map/ppermute | solution.py:249
  45.9 14.6 %collective-permute-start.5 = (bf16[64,1024]{1,0:T(8,128)(2,1)S(1)}, bf16[64,1024]{1,0:T(8,128)(2,1)S(1)}, u32[]{:S(2)}, u32[]{:S(2)}) collective-permute-start(bf16[64,1024]{1,0:T(8,128)(2,1)S(1)} %dynamic-slice_convert_fusion.refs_1_), channel_id=1, source_target_pairs={{0,24},{1,25},{2,26},{3,27},{4,28},{5,29},{6,30},{7,31},{8,0},{9,1... | collective-permute-start | bytes 393224 | tf_op jit(solution)/shard_map/ppermute | solution.py:249
  59.7 22.7 %collective-permute-start.32 = (bf16[256,1024]{1,0:T(8,128)(2,1)S(1)}, bf16[256,1024]{1,0:T(8,128)(2,1)S(1)}, u32[]{:S(2)}, u32[]{:S(2)}) collective-permute-start(bf16[256,1024]{1,0:T(8,128)(2,1)S(1)} %convert_element_type.16.refs_4_.refs_11_.refs_6_), channel_id=1, source_target_pairs={{0,1},{1,0},{2,3},{3,2},{4,5},{5,4},{6,7},{7,6},{8,9},{9,8},{10,11... | collective-permute-start | bytes 1572872 | tf_op jit(solution)/shard_map/ppermute | solution.py:249
  60.5 21.9 %collective-permute-start.6 = (bf16[256,1024]{1,0:T(8,128)(2,1)S(1)}, bf16[256,1024]{1,0:T(8,128)(2,1)S(1)}, u32[]{:S(2)}, u32[]{:S(2)}) collective-permute-start(bf16[256,1024]{1,0:T(8,128)(2,1)S(1)} %pad_maximum_fusion.refs_0_), channel_id=1, source_target_pairs={{0,4},{1,5},{2,6},{3,7},{4,0},{5,1},{6,2},{7,3},{8,12},{9,13},{10,... | collective-permute-start | bytes 1572872 | tf_op jit(solution)/shard_map/ppermute | solution.py:249
  62.1 12.6 %collective-permute-start.19 = (bf16[64,1152]{1,0:T(8,128)(2,1)S(1)}, bf16[64,1152]{1,0:T(8,128)(2,1)S(1)}, u32[]{:S(2)}, u32[]{:S(2)}) collective-permute-start(bf16[64,1152]{1,0:T(8,128)(2,1)S(1)} %get-tuple-element.10), channel_id=1, source_target_pairs={{0,16},{1,17},{2,18},{3,19},{4,20},{5,21},{6,22},{7,23},{8,24},{9,... | collective-permute-start | bytes 442376 | tf_op jit(solution)/shard_map/ppermute | solution.py:249
  62.1 13.5 %collective-permute-start.20 = (bf16[64,1152]{1,0:T(8,128)(2,1)S(1)}, bf16[64,1152]{1,0:T(8,128)(2,1)S(1)}, u32[]{:S(2)}, u32[]{:S(2)}) collective-permute-start(bf16[64,1152]{1,0:T(8,128)(2,1)S(1)} %get-tuple-element.11), channel_id=1, source_target_pairs={{0,8},{1,9},{2,10},{3,11},{4,12},{5,13},{6,14},{7,15},{8,16},{9,17... | collective-permute-start | bytes 442376 | tf_op jit(solution)/shard_map/ppermute | solution.py:249
  67.2 13.7 %collective-permute-start.7 = (bf16[128,1024]{1,0:T(8,128)(2,1)S(1)}, bf16[128,1024]{1,0:T(8,128)(2,1)S(1)}, u32[]{:S(2)}, u32[]{:S(2)}) collective-permute-start(bf16[128,1024]{1,0:T(8,128)(2,1)S(1)} %pad_maximum_fusion.1), channel_id=1, source_target_pairs={{0,4},{1,5},{2,6},{3,7},{4,0},{5,1},{6,2},{7,3},{8,12},{9,13},{10,... | collective-permute-start | bytes 786440 | tf_op jit(solution)/shard_map/ppermute | solution.py:249
  74.6 10.8 %collective-permute-start.35 = (bf16[128,1024]{1,0:T(8,128)(2,1)S(1)}, bf16[128,1024]{1,0:T(8,128)(2,1)S(1)}, u32[]{:S(2)}, u32[]{:S(2)}) collective-permute-start(bf16[128,1024]{1,0:T(8,128)(2,1)S(1)} %slice.23), channel_id=1, source_target_pairs={{0,4},{1,5},{2,6},{3,7},{4,0},{5,1},{6,2},{7,3},{8,12},{9,13},{10,... | collective-permute-start | bytes 786440 | tf_op jit(solution)/shard_map/ppermute | solution.py:249
  75.7 9.8 %collective-permute-start.36 = (bf16[128,1024]{1,0:T(8,128)(2,1)S(1)}, bf16[128,1024]{1,0:T(8,128)(2,1)S(1)}, u32[]{:S(2)}, u32[]{:S(2)}) collective-permute-start(bf16[128,1024]{1,0:T(8,128)(2,1)S(1)} %slice.24), channel_id=1, source_target_pairs={{0,2},{1,3},{2,0},{3,1},{4,6},{5,7},{6,4},{7,5},{8,10},{9,11},{10,... | collective-permute-start | bytes 786440 | tf_op jit(solution)/shard_map/ppermute | solution.py:249
  82.4 18.1 %collective-permute-start.37 = (bf16[256,1024]{1,0:T(8,128)(2,1)S(1)}, bf16[256,1024]{1,0:T(8,128)(2,1)S(1)}, u32[]{:S(2)}, u32[]{:S(2)}) collective-permute-start(bf16[256,1024]{1,0:T(8,128)(2,1)S(1)} %collective-permute-done.33.refs_6_), channel_id=1, source_target_pairs={{0,1},{1,0},{2,3},{3,2},{4,5},{5,4},{6,7},{7,6},{8,9},{9,8},{10,11... | collective-permute-start | bytes 1572872 | tf_op jit(solution)/shard_map/ppermute | solution.py:249
  85.5 16.2 %collective-permute-start.38 = (bf16[256,1024]{1,0:T(8,128)(2,1)S(1)}, bf16[256,1024]{1,0:T(8,128)(2,1)S(1)}, u32[]{:S(2)}, u32[]{:S(2)}) collective-permute-start(bf16[256,1024]{1,0:T(8,128)(2,1)S(1)} %collective-permute-done.34.refs_7_), channel_id=1, source_target_pairs={{0,1},{1,0},{2,3},{3,2},{4,5},{5,4},{6,7},{7,6},{8,9},{9,8},{10,11... | collective-permute-start | bytes 1572872 | tf_op jit(solution)/shard_map/ppermute | solution.py:249
  85.5 11.4 %collective-permute-start.8 = (bf16[128,1024]{1,0:T(8,128)(2,1)S(1)}, bf16[128,1024]{1,0:T(8,128)(2,1)S(1)}, u32[]{:S(2)}, u32[]{:S(2)}) collective-permute-start(bf16[128,1024]{1,0:T(8,128)(2,1)S(1)} %slice.20), channel_id=1, source_target_pairs={{0,2},{1,3},{2,0},{3,1},{4,6},{5,7},{6,4},{7,5},{8,10},{9,11},{10,... | collective-permute-start | bytes 786440 | tf_op jit(solution)/shard_map/ppermute | solution.py:249
  96.9 35.8 %collective-permute-start.47 = (bf16[192,1024]{1,0:T(8,128)(2,1)S(1)}, bf16[192,1024]{1,0:T(8,128)(2,1)S(1)}, u32[]{:S(2)}, u32[]{:S(2)}) collective-permute-start(bf16[192,1024]{1,0:T(8,128)(2,1)S(1)} %constant_dynamic-update-slice_fusion), channel_id=1, source_target_pairs={{0,2},{1,3},{2,0},{3,1},{4,6},{5,7},{6,4},{7,5},{8,10},{9,11},{10,... | collective-permute-start | bytes 1179656 | tf_op jit(solution)/shard_map/ppermute | solution.py:249
  97.5 35.2 %collective-permute-start.49 = (bf16[192,1024]{1,0:T(8,128)(2,1)S(1)}, bf16[192,1024]{1,0:T(8,128)(2,1)S(1)}, u32[]{:S(2)}, u32[]{:S(2)}) collective-permute-start(bf16[192,1024]{1,0:T(8,128)(2,1)S(1)} %constant_dynamic-update-slice_fusion), channel_id=1, source_target_pairs={{0,4},{1,5},{2,6},{3,7},{4,0},{5,1},{6,2},{7,3},{8,12},{9,13},{10,... | collective-permute-start | bytes 1179656 | tf_op jit(solution)/shard_map/ppermute | solution.py:249
  99.0 10.0 %collective-permute-start.21 = (f32[1,256]{1,0:T(1,128)S(1)}, f32[1,256]{1,0:T(1,128)S(1)}, u32[]{:S(2)}, u32[]{:S(2)}) collective-permute-start(f32[1,256]{1,0:T(1,128)S(1)} %get-tuple-element.12.refs_8_), channel_id=1, source_target_pairs={{0,2},{1,3},{2,0},{3,1},{4,6},{5,7},{6,4},{7,5},{8,10},{9,11},{10,... | collective-permute-start | bytes 3080 | tf_op jit(solution)/shard_map/ppermute | solution.py:249
  100.5 10.0 %collective-permute-start.22 = (f32[1,256]{1,0:T(1,128)S(1)}, f32[1,256]{1,0:T(1,128)S(1)}, u32[]{:S(2)}, u32[]{:S(2)}) collective-permute-start(f32[1,256]{1,0:T(1,128)S(1)} %get-tuple-element.12.refs_8_), channel_id=1, source_target_pairs={{0,4},{1,5},{2,6},{3,7},{4,0},{5,1},{6,2},{7,3},{8,12},{9,13},{10,... | collective-permute-start | bytes 3080 | tf_op jit(solution)/shard_map/ppermute | solution.py:249
  101.7 26.9 %collective-permute-start.46 = (bf16[64,1024]{1,0:T(8,128)(2,1)S(1)}, bf16[64,1024]{1,0:T(8,128)(2,1)S(1)}, u32[]{:S(2)}, u32[]{:S(2)}) collective-permute-start(bf16[64,1024]{1,0:T(8,128)(2,1)S(1)} %get-tuple-element.13.refs_0_), channel_id=1, source_target_pairs={{0,2},{1,3},{2,0},{3,1},{4,6},{5,7},{6,4},{7,5},{8,10},{9,11},{10,... | collective-permute-start | bytes 393224 | tf_op jit(solution)/shard_map/ppermute | solution.py:249
  109.0 20.1 %collective-permute-start.48 = (bf16[64,1024]{1,0:T(8,128)(2,1)S(1)}, bf16[64,1024]{1,0:T(8,128)(2,1)S(1)}, u32[]{:S(2)}, u32[]{:S(2)}) collective-permute-start(bf16[64,1024]{1,0:T(8,128)(2,1)S(1)} %get-tuple-element.13.refs_0_), channel_id=1, source_target_pairs={{0,4},{1,5},{2,6},{3,7},{4,0},{5,1},{6,2},{7,3},{8,12},{9,13},{10,... | collective-permute-start | bytes 393224 | tf_op jit(solution)/shard_map/ppermute | solution.py:249
  128.5 27.1 %collective-permute-start.24 = (f32[256,1152]{1,0:T(8,128)S(1)}, f32[256,1152]{1,0:T(8,128)S(1)}, u32[]{:S(2)}, u32[]{:S(2)}) collective-permute-start(f32[256,1152]{1,0:T(8,128)S(1)} %sums.5), channel_id=1, source_target_pairs={{0,1},{1,0},{2,3},{3,2},{4,5},{5,4},{6,7},{7,6},{8,9},{9,8},{10,11... | collective-permute-start | bytes 3538952 | tf_op jit(solution)/shard_map/ppermute | solution.py:249
  134.2 24.3 %collective-permute-start.52 = (f32[256,1152]{1,0:T(8,128)S(1)}, f32[256,1152]{1,0:T(8,128)S(1)}, u32[]{:S(2)}, u32[]{:S(2)}) collective-permute-start(f32[256,1152]{1,0:T(8,128)S(1)} %sums.8), channel_id=1, source_target_pairs={{0,1},{1,0},{2,3},{3,2},{4,5},{5,4},{6,7},{7,6},{8,9},{9,8},{10,11... | collective-permute-start | bytes 3538952 | tf_op jit(solution)/shard_map/ppermute | solution.py:249
  134.3 12.4 %collective-permute-start.29 = (bf16[192,1024]{1,0:T(8,128)(2,1)S(1)}, bf16[192,1024]{1,0:T(8,128)(2,1)S(1)}, u32[]{:S(2)}, u32[]{:S(2)}) collective-permute-start(bf16[192,1024]{1,0:T(8,128)(2,1)S(1)} %constant_dynamic-update-slice_fusion), channel_id=1, source_target_pairs={{0,6},{1,7},{2,4},{3,5},{4,2},{5,3},{6,0},{7,1},{8,14},{9,15},{10,... | collective-permute-start | bytes 1179656 | tf_op jit(solution)/shard_map/ppermute | solution.py:249
  146.7 11.8 %collective-permute-start.31 = (bf16[192,1024]{1,0:T(8,128)(2,1)S(1)}, bf16[192,1024]{1,0:T(8,128)(2,1)S(1)}, u32[]{:S(2)}, u32[]{:S(2)}) collective-permute-start(bf16[192,1024]{1,0:T(8,128)(2,1)S(1)} %collective-permute-done.29.refs_1_), channel_id=1, source_target_pairs={{0,1},{1,0},{2,3},{3,2},{4,5},{5,4},{6,7},{7,6},{8,9},{9,8},{10,11... | collective-permute-start | bytes 1179656 | tf_op jit(solution)/shard_map/ppermute | solution.py:249
  (38 other events, 256.4 us)
where the time goes:
time: 161 us; the launch traced here: 160 us
  waiting for transfers between devices  78.8 us (49%)
  starting transfers between devices  49.5 us (31%)
  Pallas kernels  17.9 us (11%)
  local copies, waits for them, and re-layouts  10.2 us (6%)
  other arithmetic  2.39 us (1%)
  between operations  1.62 us (1%)
    ppermute x53, waiting for transfers between devices, shift(): return lax.ppermute(value, axes, pairs)  78.8 us
    ppermute x53, starting transfers between devices, shift(): return lax.ppermute(value, axes, pairs)  49.5 us
    pallas_call x5, Pallas kernels, sums(): pl.pallas_call(functools.partial(sums_kernel, tuple((len(chunk) for chunk...  9.73 us
    pallas_call x2, Pallas kernels, attend(): pl.pallas_call(functools.partial(attend_kernel, len(rows), len(books), re...  7.67 us
    unnamed x36, local copies, waits for them, and re-layouts  7.19 us
  transfers between devices with their start and end apart: 53, of which 21 were waited for; matrix products, arithmetic and copies ran while one was open for 3% of the time, Pallas kernels for 10%

commit v1 on v0

--- a/solution.py
+++ b/solution.py
@@ -34,15 +34,43 @@
     return high, middle, rest - middle
 
 
+def in_lanes(levels):
+    lane = lax.broadcasted_iota(jnp.int32, levels[0][0].shape, 1)
+    tail = jnp.zeros(levels[0][0].shape, F32)
+    for t, parts in enumerate(levels):
+        for n, part in enumerate(parts):
+            tail = jnp.where(lane == 3 * t + n, part, tail)
+    return tail.astype(BF)
+
+
 def attend_kernel(n_rows, n_books, rebuild, *refs):
     row_refs, book_refs = refs[:n_rows], refs[n_rows : n_rows + n_books]
-    outs, (rows, score) = refs[n_rows + n_books : -2], refs[-2:]
+    outs, (rows, score, joint) = refs[n_rows + n_books : -3], refs[-3:]
     part = row_refs[0].shape[0]
     for j in range(n_rows):
         rows[j * part : (j + 1) * part, :] = row_refs[j][...]
+    groups = [[]]
+    for ref in book_refs:
+        if sum(r.shape[0] for r in groups[-1]) + ref.shape[0] > joint.shape[1]:
+            groups.append([])
+        groups[-1].append(ref)
+    blocks = []
+    for n, group in enumerate(groups):
+        at = 0
+        if len(group) > 1:
+            for ref in group:
+                joint[n, at : at + ref.shape[0], :] = ref[...]
+                at += ref.shape[0]
+        blocks.append((group[0], None) if len(group) == 1 else (joint, (n, at)))
+
+    def block(j):
+        ref, where = blocks[j]
+        return ref[...] if where is None else ref[where[0], : where[1], :]
+
+    sizes = [sum(r.shape[0] for r in group) for group in groups]
     peak = None
-    for j in range(n_books):
-        book = book_refs[j][...]
+    for j in range(len(blocks)):
+        book = block(j)
         s = lax.dot_general(rows[...], book, NT, preferred_element_type=F32)
         s = s - as_row(half_column(book))
         score[j, :, : s.shape[1]] = s
@@ -50,12 +78,12 @@
         peak = top if peak is None else jnp.maximum(peak, top)
     total = None
     rebuilt = None
-    for j in range(n_books):
-        expo = jnp.exp(score[j, :, : book_refs[j].shape[0]] - peak)
+    for j in range(len(blocks)):
+        expo = jnp.exp(score[j, :, : sizes[j]] - peak)
         mass = jnp.sum(expo, axis=1, keepdims=True)
         total = mass if total is None else total + mass
         if rebuild:
-            term = lax.dot_general(expo.astype(BF), book_refs[j][...], NN, preferred_element_type=F32)
+            term = lax.dot_general(expo.astype(BF), block(j), NN, preferred_element_type=F32)
             rebuilt = term if rebuilt is None else rebuilt + term
     level = peak + jnp.log(total)
     if not rebuild:
@@ -66,17 +94,12 @@
         return
     width = rebuilt.shape[1]
     rebuilt = rebuilt / total
-    parts = split(level)
-    lane = lax.broadcasted_iota(jnp.int32, (part, EXTRA), 1)
+    parts = split(jnp.broadcast_to(level, (level.shape[0], EXTRA)))
     for j in range(n_rows):
         here = slice(j * part, (j + 1) * part)
         outs[j][:, :width] = rebuilt[here].astype(BF)
-        tail = jnp.zeros((part, EXTRA), F32)
-        for t in range(n_rows):
-            m = (j + t) % n_rows
-            for n, value in enumerate(parts):
-                tail = jnp.where(lane == 3 * t + n, value[m * part : (m + 1) * part], tail)
-        outs[j][:, width:] = tail.astype(BF)
+        turned = [(j + t) % n_rows for t in range(n_rows)]
+        outs[j][:, width:] = in_lanes([[p[m * part : (m + 1) * part] for p in parts] for m in turned])
 
 
 def attend(rows, books, part, weight=None):
@@ -101,6 +124,7 @@
         scratch_shapes=[
             pltpu.VMEM((frames, width), BF),
             pltpu.VMEM((len(books), frames, entries), F32),
+            pltpu.VMEM((len(books), entries, width), BF),
         ],
         compiler_params=pltpu.CompilerParams(vmem_limit_bytes=BYTES),
         cost_estimate=pl.CostEstimate(
@@ -118,18 +142,23 @@
 
 
 def combine_kernel(n, *refs):
-    frame_ref, piece_refs, (second_ref, level_ref) = refs[0], refs[1 : 1 + n], refs[1 + n :]
+    frame_ref, piece_refs, (second_ref, ahead_ref, level_ref) = refs[0], refs[1 : 1 + n], refs[1 + n :]
     part, width = frame_ref.shape
     tails = [ref[:, width:].astype(F32) for ref in piece_refs]
+    found = []
     for t in reversed(range(n)):
         parts = [tail[:, 3 * t : 3 * t + 1] + tail[:, 3 * t + 1 : 3 * t + 2] + tail[:, 3 * t + 2 : 3 * t + 3] for tail in tails]
         level = merge_levels(parts)
         level_ref[:, t * part : (t + 1) * part] = as_row(level)
+        found.insert(0, split(jnp.broadcast_to(level, (part, EXTRA))))
     rebuilt = None
     for ref, p in zip(piece_refs, parts):
         term = jnp.exp(p - level) * ref[:, :width].astype(F32)
         rebuilt = term if rebuilt is None else rebuilt + term
-    second_ref[...] = (frame_ref[...] - rebuilt).astype(BF)
+    second = (frame_ref[...] - rebuilt).astype(BF)
+    second_ref[...] = second
+    ahead_ref[:, :width] = second
+    ahead_ref[:, width:] = in_lanes(found)
 
 
 def combine(frames, pieces):
@@ -137,9 +166,13 @@
     n = len(pieces)
     return pl.pallas_call(
         functools.partial(combine_kernel, n),
-        out_shape=[jax.ShapeDtypeStruct((part, width), BF), jax.ShapeDtypeStruct((1, n * part), F32)],
+        out_shape=[
+            jax.ShapeDtypeStruct((part, width), BF),
+            jax.ShapeDtypeStruct((part, width + EXTRA), BF),
+            jax.ShapeDtypeStruct((1, n * part), F32),
+        ],
         in_specs=[pl.BlockSpec(memory_space=pltpu.VMEM)] * (1 + n),
-        out_specs=[pl.BlockSpec(memory_space=pltpu.VMEM)] * 2,
+        out_specs=[pl.BlockSpec(memory_space=pltpu.VMEM)] * 3,
         compiler_params=pltpu.CompilerParams(vmem_limit_bytes=BYTES // 4),
         cost_estimate=pl.CostEstimate(flops=4 * part * width * n, bytes_accessed=4 * part * width * n, transcendentals=0),
         name="combine",
@@ -175,7 +208,7 @@
     piece_refs, rest = refs[:n_pieces], refs[n_pieces:]
     stat_refs, rest = rest[:n_chunks], rest[n_chunks:]
     book_ref, before, rest = rest[0], rest[1 : 1 + n_before], rest[1 + n_before :]
-    out_ref, hold = rest[-2:]
+    out_ref, hold, row = rest[-3:]
     book = book_ref[...]
     width = book.shape[1]
     half = half_column(book)
@@ -188,12 +221,21 @@
         else:
             row_at = 0
             for ref in piece_refs[at : at + count]:
-                hold[j % 2, row_at : row_at + ref.shape[0], :] = ref[...]
+                hold[j % 2, row_at : row_at + ref.shape[0], :] = ref[:, :width]
                 row_at += ref.shape[0]
             chunk = hold[j % 2]
         at += count
         s = lax.dot_general(book, chunk, NT, preferred_element_type=F32) - half
-        prob = jnp.exp(s - stat_refs[j][...])
+        stat = stat_refs[j]
+        if stat.shape[0] == 1:
+            level = stat[...]
+        else:
+            part = stat.shape[0]
+            turned = stat[:, width:].astype(F32).T
+            for t in range(row.shape[1] // part):
+                row[j % 8 : j % 8 + 1, t * part : (t + 1) * part] = sum(turned[3 * t + n : 3 * t + n + 1] for n in (1, 2)) + turned[3 * t : 3 * t + 1]
+            level = row[j % 8 : j % 8 + 1, :]
+        prob = jnp.exp(s - level)
         mass = jnp.sum(prob, axis=1, keepdims=True)
         term = lax.dot_general(prob.astype(BF), chunk, NN, preferred_element_type=F32)
         num = term if num is None else num + term
@@ -213,13 +255,14 @@
     pieces = [piece for chunk in chunks for piece in chunk]
     frames = sum(piece.shape[0] for piece in pieces)
     codes = () if code is None else (code,)
+    many = sum(piece.shape[0] for piece in chunks[0])
     ins = (*pieces, *stats, book, *before, *codes)
     return pl.pallas_call(
         functools.partial(sums_kernel, tuple(len(chunk) for chunk in chunks), len(before), bool(codes)),
         out_shape=jax.ShapeDtypeStruct((entries, width + (0 if codes else EXTRA)), F32),
         in_specs=[pl.BlockSpec(memory_space=pltpu.VMEM)] * len(ins),
         out_specs=pl.BlockSpec(memory_space=pltpu.VMEM),
-        scratch_shapes=[pltpu.VMEM((2, stats[0].shape[1], width), BF)],
+        scratch_shapes=[pltpu.VMEM((2, many, width), BF), pltpu.VMEM((8, many), F32)],
         compiler_params=pltpu.CompilerParams(vmem_limit_bytes=BYTES),
         cost_estimate=pl.CostEstimate(
             flops=4 * frames * entries * width,
@@ -303,11 +346,11 @@
         else:
             weight = jnp.repeat((depth == 2).astype(F32), group)
             weight = lax.dynamic_slice_in_dim(weight, starts[0], part, 0).reshape(1, part)
-        second, level = combine(rows[0], returned)
+        second, message, level = combine(rows[0], returned)
 
         seconds = [second] + [shift(second, z=j) for j in range(1, lz)]
-        ahead = spread(second)
-        stats = [level] + spread(level)
+        ahead = spread(message)
+        stats = [level] + ahead
         rest = spread(jnp.concatenate(seconds[1:], 0))
         chunks_two = [seconds] + [list(chunk) for chunk in zip(ahead, rest)]
         (note,) = attend(seconds, near_two + far_two, part, weight)
@@ -319,12 +362,13 @@
 
         stats = stats_of(notes, part)
         stats = [stats] + spread(stats)
-        early = [sums(chunks_two[:-1], stats[:-1], near_two[m]) for m in range(lc)]
-        sent = [shift(other, c=-m) for m, other in enumerate(early[1:], 1)]
+        others = [sums(chunks_two[:-1], stats[:-1], near_two[m]) for m in range(1, lc)]
+        sent = [shift(other, c=-m) for m, other in enumerate(others, 1)]
+        early = sums(chunks_two[:-1], stats[:-1], near_two[0])
         last = [chunks_two[-1][0], chunks_two[-1][1]]
         last = [last] + [[shift(last[0], c=m), shift(last[1], c=m)] for m in range(1, lc)]
         stats = [stats[-1]] + [shift(stats[-1], c=m) for m in range(1, lc)]
-        new_two = sums(last, stats, near_two[0], [early[0]] + sent, code_two)
+        new_two = sums(last, stats, near_two[0], [early] + sent, code_two)
         return new_one, new_two
 
     return on_device

time: 161 us -> 143 us (0.89)
  waiting for transfers between devices: 78.8 us -> 66.5 us
  local copies, waits for them, and re-layouts: 10.2 us -> 3.04 us
  starting transfers between devices: 49.5 us -> 51.8 us
    ppermute x53 -> x50, waiting for transfers between devices: 78.8 us -> 66.5 us  [shift(): return lax.ppermute(value, axes, pairs)]
    unnamed x36 -> x10, local copies, waits for them, and re-layouts: 7.19 us -> 0.04 us
    ppermute x53 -> x50, starting transfers between devices: 49.5 us -> 51.8 us  [shift(): return lax.ppermute(value, axes, pairs)]
  transfers between devices with their start and end apart: 53 -> 50, of which waited for: 21 -> 21; matrix products, arithmetic and copies ran while one was open for 3% -> 4% of each run, Pallas kernels for 10% -> 10%
where the time goes in v1:
time: 143 us
  waiting for transfers between devices  66.5 us (47%)
  starting transfers between devices  51.8 us (36%)
  Pallas kernels  16.9 us (12%)
  other arithmetic  3.45 us (2%)
  local copies, waits for them, and re-layouts  3.04 us (2%)
  between operations  1.57 us (1%)
    ppermute x50, waiting for transfers between devices, shift(): return lax.ppermute(value, axes, pairs)  66.5 us
    ppermute x50, starting transfers between devices, shift(): return lax.ppermute(value, axes, pairs)  51.8 us
    pallas_call x5, Pallas kernels, sums(): pl.pallas_call(functools.partial(sums_kernel, tuple((len(chunk) for chunk...  9.75 us
    pallas_call x2, Pallas kernels, attend(): pl.pallas_call(functools.partial(attend_kernel, len(rows), len(books), re...  6.61 us
  transfers between devices with their start and end apart: 50, of which 21 were waited for; matrix products, arithmetic and copies ran while one was open for 4% of the time, Pallas kernels for 10%

profile of v1, /device:TPU:0, one launch (start us, length us, event | category | flops | bytes accessed | tf_op | source)
XLA Modules:
  0.0 143.2 jit_solution(12177554275754572112)
XLA Ops:
  2.0 3.1 %collective-permute-start.10 = (bf16[256,1024]{1,0:T(8,128)(2,1)S(1)}, bf16[256,1024]{1,0:T(8,128)(2,1)}, u32[]{:S(2)}, u32[]{:S(2)}) collective-permute-start(bf16[256,1024]{1,0:T(8,128)(2,1)S(1)} %convert_element_type.15.refs_4_.refs_12_), channel_id=1, source_target_pairs={{0,2},{1,3},{2,0},{3,1},{4,6},{5,7},{6,4},{7,5},{8,10},{9,11},{10,... | collective-permute-start | bytes 1572872 | tf_op jit(solution)/shard_map/ppermute | solution.py:292
  7.6 1.6 %collective-permute-start = (bf16[64,1024]{1,0:T(8,128)(2,1)S(1)}, bf16[64,1024]{1,0:T(8,128)(2,1)S(1)}, u32[]{:S(2)}, u32[]{:S(2)}) collective-permute-start(bf16[64,1024]{1,0:T(8,128)(2,1)S(1)} %get-tuple-element.16.refs_0_), channel_id=1, source_target_pairs={{0,8},{1,9},{2,10},{3,11},{4,12},{5,13},{6,14},{7,15},{8,16},{9,17... | collective-permute-start | bytes 393224 | tf_op jit(solution)/shard_map/ppermute | solution.py:292
  9.2 2.6 %collective-permute-start.1 = (bf16[64,1024]{1,0:T(8,128)(2,1)S(1)}, bf16[64,1024]{1,0:T(8,128)(2,1)}, u32[]{:S(2)}, u32[]{:S(2)}) collective-permute-start(bf16[64,1024]{1,0:T(8,128)(2,1)S(1)} %get-tuple-element.16.refs_0_), channel_id=1, source_target_pairs={{0,16},{1,17},{2,18},{3,19},{4,20},{5,21},{6,22},{7,23},{8,24},{9,... | collective-permute-start | bytes 393224 | tf_op jit(solution)/shard_map/ppermute | solution.py:292
  11.9 4.0 %collective-permute-done.refs_1_ = bf16[64,1024]{1,0:T(8,128)(2,1)S(1)} collective-permute-done((bf16[64,1024]{1,0:T(8,128)(2,1)S(1)}, bf16[64,1024]{1,0:T(8,128)(2,1)S(1)}, u32[]{:S(2)}, u32[]{:S(2)}) %collective-permute-start) | collective-permute-done | bytes 131104 | tf_op jit(solution)/shard_map/ppermute | solution.py:292
  17.3 1.6 %collective-permute-start.32 = (bf16[256,1024]{1,0:T(8,128)(2,1)S(1)}, bf16[256,1024]{1,0:T(8,128)(2,1)S(1)}, u32[]{:S(2)}, u32[]{:S(2)}) collective-permute-start(bf16[256,1024]{1,0:T(8,128)(2,1)S(1)} %convert_element_type.16.refs_4_.refs_11_.refs_6_), channel_id=1, source_target_pairs={{0,2},{1,3},{2,0},{3,1},{4,6},{5,7},{6,4},{7,5},{8,10},{9,11},{10,... | collective-permute-start | bytes 1572872 | tf_op jit(solution)/shard_map/ppermute | solution.py:292
  24.5 3.1 %collective-permute-start.4 = (bf16[64,1024]{1,0:T(8,128)(2,1)S(1)}, bf16[64,1024]{1,0:T(8,128)(2,1)S(1)}, u32[]{:S(2)}, u32[]{:S(2)}) collective-permute-start(bf16[64,1024]{1,0:T(8,128)(2,1)S(1)} %dynamic-slice_convert_fusion.refs_1_), channel_id=1, source_target_pairs={{0,16},{1,17},{2,18},{3,19},{4,20},{5,21},{6,22},{7,23},{8,24},{9,... | collective-permute-start | bytes 393224 | tf_op jit(solution)/shard_map/ppermute | solution.py:292
  28.7 3.0 %collective-permute-done.3.refs_2_ = bf16[64,1024]{1,0:T(8,128)(2,1)S(1)} collective-permute-done((bf16[64,1024]{1,0:T(8,128)(2,1)S(1)}, bf16[64,1024]{1,0:T(8,128)(2,1)S(1)}, u32[]{:S(2)}, u32[]{:S(2)}) %collective-permute-start.3) | collective-permute-done | bytes 131104 | tf_op jit(solution)/shard_map/ppermute | solution.py:292
  32.1 3.6 %collective-permute-done.4.refs_3_ = bf16[64,1024]{1,0:T(8,128)(2,1)S(1)} collective-permute-done((bf16[64,1024]{1,0:T(8,128)(2,1)S(1)}, bf16[64,1024]{1,0:T(8,128)(2,1)S(1)}, u32[]{:S(2)}, u32[]{:S(2)}) %collective-permute-start.4) | collective-permute-done | bytes 131104 | tf_op jit(solution)/shard_map/ppermute | solution.py:292
  40.8 2.3 %collective-permute-start.5 = (bf16[64,1024]{1,0:T(8,128)(2,1)S(1)}, bf16[64,1024]{1,0:T(8,128)(2,1)S(1)}, u32[]{:S(2)}, u32[]{:S(2)}) collective-permute-start(bf16[64,1024]{1,0:T(8,128)(2,1)S(1)} %dynamic-slice_convert_fusion.refs_1_), channel_id=1, source_target_pairs={{0,24},{1,25},{2,26},{3,27},{4,28},{5,29},{6,30},{7,31},{8,0},{9,1... | collective-permute-start | bytes 393224 | tf_op jit(solution)/shard_map/ppermute | solution.py:292
  43.5 4.6 %attend.1 = (bf16[64,1152]{1,0:T(8,128)(2,1)S(1)}, bf16[64,1152]{1,0:T(8,128)(2,1)S(1)}, bf16[64,1152]{1,0:T(8,128)(2,1)S(1)}, bf16[64,1152]{1,0:T(8,128)(2,1)S(1)}) custom-call(bf16[64,1024]{1,0:T(8,128)(2,1)S(1)} %get-tuple-element.16.refs_0_, bf16[64,1024]{1,0:T(8,128)(2,1)S(1)} %copy-done.3, bf16[64,1024]{1,0:T(8,128)(2,1)} %collective-permute-done.1.refs_2_, ...), custom_call_target="tpu_custom_call" | custom-call | flops 2147483648 | bytes 4718592 | tf_op jit(solution)/shard_map/attend/pallas_call | solution.py:117
  48.1 2.6 %collective-permute-start.18 = (bf16[64,1152]{1,0:T(8,128)(2,1)S(1)}, bf16[64,1152]{1,0:T(8,128)(2,1)S(1)}, u32[]{:S(2)}, u32[]{:S(2)}) collective-permute-start(bf16[64,1152]{1,0:T(8,128)(2,1)S(1)} %get-tuple-element.10), channel_id=1, source_target_pairs={{0,24},{1,25},{2,26},{3,27},{4,28},{5,29},{6,30},{7,31},{8,0},{9,1... | collective-permute-start | bytes 442376 | tf_op jit(solution)/shard_map/ppermute | solution.py:292
  51.2 11.2 %collective-permute-done.6.refs_5_ = bf16[256,1024]{1,0:T(8,128)(2,1)S(1)} collective-permute-done((bf16[256,1024]{1,0:T(8,128)(2,1)S(1)}, bf16[256,1024]{1,0:T(8,128)(2,1)S(1)}, u32[]{:S(2)}, u32[]{:S(2)}) %collective-permute-start.6) | collective-permute-done | bytes 524320 | tf_op jit(solution)/shard_map/ppermute | solution.py:292
  63.9 4.1 %collective-permute-done.34.refs_8_ = bf16[128,1024]{1,0:T(8,128)(2,1)S(1)} collective-permute-done((bf16[128,1024]{1,0:T(8,128)(2,1)S(1)}, bf16[128,1024]{1,0:T(8,128)(2,1)S(1)}, u32[]{:S(2)}, u32[]{:S(2)}) %collective-permute-start.34) | collective-permute-done | bytes 262176 | tf_op jit(solution)/shard_map/ppermute | solution.py:292
  68.6 1.6 %collective-permute-start.8 = (bf16[128,1024]{1,0:T(8,128)(2,1)S(1)}, bf16[128,1024]{1,0:T(8,128)(2,1)S(1)}, u32[]{:S(2)}, u32[]{:S(2)}) collective-permute-start(bf16[128,1024]{1,0:T(8,128)(2,1)S(1)} %slice.20), channel_id=1, source_target_pairs={{0,2},{1,3},{2,0},{3,1},{4,6},{5,7},{6,4},{7,5},{8,10},{9,11},{10,... | collective-permute-start | bytes 786440 | tf_op jit(solution)/shard_map/ppermute | solution.py:292
  70.2 4.7 %collective-permute-done.20.refs_4_ = bf16[64,1152]{1,0:T(8,128)(2,1)S(1)} collective-permute-done((bf16[64,1152]{1,0:T(8,128)(2,1)S(1)}, bf16[64,1152]{1,0:T(8,128)(2,1)S(1)}, u32[]{:S(2)}, u32[]{:S(2)}) %collective-permute-start.20) | collective-permute-done | bytes 147488 | tf_op jit(solution)/shard_map/ppermute | solution.py:292
  75.6 1.7 %collective-permute-done.35.refs_9_ = bf16[128,1024]{1,0:T(8,128)(2,1)S(1)} collective-permute-done((bf16[128,1024]{1,0:T(8,128)(2,1)S(1)}, bf16[128,1024]{1,0:T(8,128)(2,1)S(1)}, u32[]{:S(2)}, u32[]{:S(2)}) %collective-permute-start.35) | collective-permute-done | bytes 262176 | tf_op jit(solution)/shard_map/ppermute | solution.py:292
  77.3 3.8 %collective-permute-start.27 = (bf16[64,1024]{1,0:T(8,128)(2,1)S(1)}, bf16[64,1024]{1,0:T(8,128)(2,1)S(1)}, u32[]{:S(2)}, u32[]{:S(2)}) collective-permute-start(bf16[64,1024]{1,0:T(8,128)(2,1)S(1)} %get-tuple-element.15.refs_0_), channel_id=1, source_target_pairs={{0,24},{1,25},{2,26},{3,27},{4,28},{5,29},{6,30},{7,31},{8,0},{9,1... | collective-permute-start | bytes 393224 | tf_op jit(solution)/shard_map/ppermute | solution.py:292
  81.1 2.6 %collective-permute-done.25.refs_1_ = bf16[64,1024]{1,0:T(8,128)(2,1)S(1)} collective-permute-done((bf16[64,1024]{1,0:T(8,128)(2,1)S(1)}, bf16[64,1024]{1,0:T(8,128)(2,1)S(1)}, u32[]{:S(2)}, u32[]{:S(2)}) %collective-permute-start.25) | collective-permute-done | bytes 131104 | tf_op jit(solution)/shard_map/ppermute | solution.py:292
  84.4 4.1 %collective-permute-done.26.refs_2_ = bf16[64,1024]{1,0:T(8,128)(2,1)S(1)} collective-permute-done((bf16[64,1024]{1,0:T(8,128)(2,1)S(1)}, bf16[64,1024]{1,0:T(8,128)(2,1)S(1)}, u32[]{:S(2)}, u32[]{:S(2)}) %collective-permute-start.26) | collective-permute-done | bytes 131104 | tf_op jit(solution)/shard_map/ppermute | solution.py:292
  90.5 1.6 %collective-permute-start.45 = (bf16[192,1024]{1,0:T(8,128)(2,1)S(1)}, bf16[192,1024]{1,0:T(8,128)(2,1)S(1)}, u32[]{:S(2)}, u32[]{:S(2)}) collective-permute-start(bf16[192,1024]{1,0:T(8,128)(2,1)S(1)} %constant_dynamic-update-slice_fusion), channel_id=1, source_target_pairs={{0,2},{1,3},{2,0},{3,1},{4,6},{5,7},{6,4},{7,5},{8,10},{9,11},{10,... | collective-permute-start | bytes 1179656 | tf_op jit(solution)/shard_map/ppermute | solution.py:292
  92.1 3.1 %collective-permute-done.22.refs_10_.refs_6_ = bf16[64,1152]{1,0:T(8,128)(2,1)S(1)} collective-permute-done((bf16[64,1152]{1,0:T(8,128)(2,1)S(1)}, bf16[64,1152]{1,0:T(8,128)(2,1)S(1)}, u32[]{:S(2)}, u32[]{:S(2)}) %collective-permute-start.22) | collective-permute-done | bytes 147488 | tf_op jit(solution)/shard_map/ppermute | solution.py:292
  98.6 1.9 %sums.5 = f32[256,1152]{1,0:T(8,128)S(1)} custom-call(bf16[256,1024]{1,0:T(8,128)(2,1)S(1)} %pad_maximum_fusion.refs_0_, bf16[64,1024]{1,0:T(8,128)(2,1)S(1)} %dynamic-slice_convert_fusion.refs_1_, bf16[64,1024]{1,0:T(8,128)(2,1)S(1)} %collective-permute-done.3.refs_2_, bf16[64,1024]{1,0:T(8,128)(2,1)S(1)} %collective-permute-done.4.refs_3_, ...), custom_call_target="tpu_custom_call" | custom-call | flops 1073741824 | bytes 3670016 | tf_op jit(solution)/shard_map/sums/pallas_call | solution.py:260
  101.0 2.1 %levels.1.refs_0_ = f32[1,320]{1,0:T(1,128)S(1)} custom-call(bf16[64,1024]{1,0:T(8,128)(2,1)S(1)} %get-tuple-element.15.refs_0_, bf16[64,1024]{1,0:T(8,128)(2,1)S(1)} %collective-permute-done.25.refs_1_, bf16[64,1024]{1,0:T(8,128)(2,1)S(1)} %collective-permute-done.26.refs_2_, bf16[64,1024]{1,0:T(8,128)(2,1)S(1)} %collective-permute-done.27.refs_3_, ...), custom_call_target="tpu_custom_call" | custom-call | flops 1073741824 | bytes 4718592 | tf_op jit(solution)/shard_map/levels/pallas_call | solution.py:117
  104.2 2.4 %collective-permute-start.41 = (f32[1,320]{1,0:T(1,128)S(1)}, f32[1,320]{1,0:T(1,128)S(1)}, u32[]{:S(2)}, u32[]{:S(2)}) collective-permute-start(f32[1,320]{1,0:T(1,128)S(1)} %levels.1.refs_0_), channel_id=1, source_target_pairs={{0,16},{1,17},{2,18},{3,19},{4,20},{5,21},{6,22},{7,23},{8,24},{9,... | collective-permute-start | bytes 3848 | tf_op jit(solution)/shard_map/ppermute | solution.py:292
  106.7 1.8 %collective-permute-done.40.refs_1_ = f32[1,320]{1,0:T(1,128)S(1)} collective-permute-done((f32[1,320]{1,0:T(1,128)S(1)}, f32[1,320]{1,0:T(1,128)S(1)}, u32[]{:S(2)}, u32[]{:S(2)}) %collective-permute-start.40) | collective-permute-done | bytes 1312 | tf_op jit(solution)/shard_map/ppermute | solution.py:292
  109.7 2.4 %collective-permute-done.42.refs_3_ = f32[1,320]{1,0:T(1,128)S(1)} collective-permute-done((f32[1,320]{1,0:T(1,128)S(1)}, f32[1,320]{1,0:T(1,128)S(1)}, u32[]{:S(2)}, u32[]{:S(2)}) %collective-permute-start.42) | collective-permute-done | bytes 1312 | tf_op jit(solution)/shard_map/ppermute | solution.py:292
  112.2 2.0 %collective-permute-start.47 = (f32[1,256]{1,0:T(1,128)S(1)}, f32[1,256]{1,0:T(1,128)S(1)}, u32[]{:S(2)}, u32[]{:S(2)}) collective-permute-start(f32[1,256]{1,0:T(1,128)S(1)} %stats.1.refs_8_), channel_id=1, source_target_pairs={{0,2},{1,3},{2,0},{3,1},{4,6},{5,7},{6,4},{7,5},{8,10},{9,11},{10,... | collective-permute-start | bytes 3080 | tf_op jit(solution)/shard_map/ppermute | solution.py:292
  115.8 1.9 %collective-permute-done.48.refs_10_ = f32[1,256]{1,0:T(1,128)S(1)} collective-permute-done((f32[1,256]{1,0:T(1,128)S(1)}, f32[1,256]{1,0:T(1,128)S(1)}, u32[]{:S(2)}, u32[]{:S(2)}) %collective-permute-start.48) | collective-permute-done | bytes 1056 | tf_op jit(solution)/shard_map/ppermute | solution.py:292
  120.8 10.9 %collective-permute-done.28.refs_1_ = bf16[192,1024]{1,0:T(8,128)(2,1)S(1)} collective-permute-done((bf16[192,1024]{1,0:T(8,128)(2,1)S(1)}, bf16[192,1024]{1,0:T(8,128)(2,1)S(1)}, u32[]{:S(2)}, u32[]{:S(2)}) %collective-permute-start.28) | collective-permute-done | bytes 393248 | tf_op jit(solution)/shard_map/ppermute | solution.py:292
  133.2 3.0 %collective-permute-done.43.refs_4_ = f32[1,256]{1,0:T(1,128)S(1)} collective-permute-done((f32[1,256]{1,0:T(1,128)S(1)}, f32[1,256]{1,0:T(1,128)S(1)}, u32[]{:S(2)}, u32[]{:S(2)}) %collective-permute-start.43) | collective-permute-done | bytes 1056 | tf_op jit(solution)/shard_map/ppermute | solution.py:292
  138.2 2.9 %sums.6 = f32[256,1024]{1,0:T(8,128)} custom-call(bf16[256,1024]{1,0:T(8,128)(2,1)S(1)} %pad_maximum_fusion.refs_0_, bf16[64,1024]{1,0:T(8,128)(2,1)S(1)} %dynamic-slice_convert_fusion.refs_1_, bf16[64,1024]{1,0:T(8,128)(2,1)S(1)} %collective-permute-done.3.refs_2_, bf16[64,1024]{1,0:T(8,128)(2,1)S(1)} %collective-permute-done.4.refs_3_, ...), custom_call_target="tpu_custom_call" | custom-call | flops 1073741824 | bytes 3670016 | tf_op jit(solution)/shard_map/sums/pallas_call | solution.py:260
  141.2 2.0 %sums.9 = f32[256,1024]{1,0:T(8,128)} custom-call(bf16[64,1152]{1,0:T(8,128)(2,1)S(1)} %collective-permute-done.23.refs_11_.refs_0_, bf16[192,1024]{1,0:T(8,128)(2,1)S(1)} %collective-permute-done.28.refs_1_, bf16[64,1152]{1,0:T(8,128)(2,1)S(1)} %collective-permute-done.29.refs_2_, bf16[192,1024]{1,0:T(8,128)(2,1)S(1)} %collective-permute-done.30.refs_3_, ...), custom_call_target="tpu_custom_call" | custom-call | flops 536870912 | bytes 2621440 | tf_op jit(solution)/shard_map/sums/pallas_call | solution.py:260
  (100 shorter events, 37.5 us)
Async XLA Ops:
  2.0 15.3 %collective-permute-start.10 = (bf16[256,1024]{1,0:T(8,128)(2,1)S(1)}, bf16[256,1024]{1,0:T(8,128)(2,1)}, u32[]{:S(2)}, u32[]{:S(2)}) collective-permute-start(bf16[256,1024]{1,0:T(8,128)(2,1)S(1)} %convert_element_type.15.refs_4_.refs_12_), channel_id=1, source_target_pairs={{0,2},{1,3},{2,0},{3,1},{4,6},{5,7},{6,4},{7,5},{8,10},{9,11},{10,... | collective-permute-start | bytes 1572872 | tf_op jit(solution)/shard_map/ppermute | solution.py:292
  5.1 19.4 %collective-permute-start.11 = (bf16[256,1024]{1,0:T(8,128)(2,1)S(1)}, bf16[256,1024]{1,0:T(8,128)(2,1)}, u32[]{:S(2)}, u32[]{:S(2)}) collective-permute-start(bf16[256,1024]{1,0:T(8,128)(2,1)S(1)} %convert_element_type.15.refs_4_.refs_12_), channel_id=1, source_target_pairs={{0,4},{1,5},{2,6},{3,7},{4,0},{5,1},{6,2},{7,3},{8,12},{9,13},{10,... | collective-permute-start | bytes 1572872 | tf_op jit(solution)/shard_map/ppermute | solution.py:292
  6.6 29.2 %collective-permute-start.9 = (bf16[256,1024]{1,0:T(8,128)(2,1)S(1)}, bf16[256,1024]{1,0:T(8,128)(2,1)S(1)}, u32[]{:S(2)}, u32[]{:S(2)}) collective-permute-start(bf16[256,1024]{1,0:T(8,128)(2,1)S(1)} %convert_element_type.15.refs_4_.refs_12_), channel_id=1, source_target_pairs={{0,1},{1,0},{2,3},{3,2},{4,5},{5,4},{6,7},{7,6},{8,9},{9,8},{10,11... | collective-permute-start | bytes 1572872 | tf_op jit(solution)/shard_map/ppermute | solution.py:292
  7.6 8.3 %collective-permute-start = (bf16[64,1024]{1,0:T(8,128)(2,1)S(1)}, bf16[64,1024]{1,0:T(8,128)(2,1)S(1)}, u32[]{:S(2)}, u32[]{:S(2)}) collective-permute-start(bf16[64,1024]{1,0:T(8,128)(2,1)S(1)} %get-tuple-element.16.refs_0_), channel_id=1, source_target_pairs={{0,8},{1,9},{2,10},{3,11},{4,12},{5,13},{6,14},{7,15},{8,16},{9,17... | collective-permute-start | bytes 393224 | tf_op jit(solution)/shard_map/ppermute | solution.py:292
  9.2 12.0 %collective-permute-start.1 = (bf16[64,1024]{1,0:T(8,128)(2,1)S(1)}, bf16[64,1024]{1,0:T(8,128)(2,1)}, u32[]{:S(2)}, u32[]{:S(2)}) collective-permute-start(bf16[64,1024]{1,0:T(8,128)(2,1)S(1)} %get-tuple-element.16.refs_0_), channel_id=1, source_target_pairs={{0,16},{1,17},{2,18},{3,19},{4,20},{5,21},{6,22},{7,23},{8,24},{9,... | collective-permute-start | bytes 393224 | tf_op jit(solution)/shard_map/ppermute | solution.py:292
  15.9 7.5 %collective-permute-start.2 = (bf16[64,1024]{1,0:T(8,128)(2,1)S(1)}, bf16[64,1024]{1,0:T(8,128)(2,1)}, u32[]{:S(2)}, u32[]{:S(2)}) collective-permute-start(bf16[64,1024]{1,0:T(8,128)(2,1)S(1)} %get-tuple-element.16.refs_0_), channel_id=1, source_target_pairs={{0,24},{1,25},{2,26},{3,27},{4,28},{5,29},{6,30},{7,31},{8,0},{9,1... | collective-permute-start | bytes 393224 | tf_op jit(solution)/shard_map/ppermute | solution.py:292
  17.3 19.1 %collective-permute-start.32 = (bf16[256,1024]{1,0:T(8,128)(2,1)S(1)}, bf16[256,1024]{1,0:T(8,128)(2,1)S(1)}, u32[]{:S(2)}, u32[]{:S(2)}) collective-permute-start(bf16[256,1024]{1,0:T(8,128)(2,1)S(1)} %convert_element_type.16.refs_4_.refs_11_.refs_6_), channel_id=1, source_target_pairs={{0,2},{1,3},{2,0},{3,1},{4,6},{5,7},{6,4},{7,5},{8,10},{9,11},{10,... | collective-permute-start | bytes 1572872 | tf_op jit(solution)/shard_map/ppermute | solution.py:292
  21.2 15.1 %collective-permute-start.12 = (bf16[128,1024]{1,0:T(8,128)(2,1)S(1)}, bf16[128,1024]{1,0:T(8,128)(2,1)S(1)}, u32[]{:S(2)}, u32[]{:S(2)}) collective-permute-start(bf16[128,1024]{1,0:T(8,128)(2,1)S(1)} %slice.21), channel_id=1, source_target_pairs={{0,4},{1,5},{2,6},{3,7},{4,0},{5,1},{6,2},{7,3},{8,12},{9,13},{10,... | collective-permute-start | bytes 786440 | tf_op jit(solution)/shard_map/ppermute | solution.py:292
  23.4 8.3 %collective-permute-start.3 = (bf16[64,1024]{1,0:T(8,128)(2,1)S(1)}, bf16[64,1024]{1,0:T(8,128)(2,1)S(1)}, u32[]{:S(2)}, u32[]{:S(2)}) collective-permute-start(bf16[64,1024]{1,0:T(8,128)(2,1)S(1)} %dynamic-slice_convert_fusion.refs_1_), channel_id=1, source_target_pairs={{0,8},{1,9},{2,10},{3,11},{4,12},{5,13},{6,14},{7,15},{8,16},{9,17... | collective-permute-start | bytes 393224 | tf_op jit(solution)/shard_map/ppermute | solution.py:292
  24.5 11.2 %collective-permute-start.4 = (bf16[64,1024]{1,0:T(8,128)(2,1)S(1)}, bf16[64,1024]{1,0:T(8,128)(2,1)S(1)}, u32[]{:S(2)}, u32[]{:S(2)}) collective-permute-start(bf16[64,1024]{1,0:T(8,128)(2,1)S(1)} %dynamic-slice_convert_fusion.refs_1_), channel_id=1, source_target_pairs={{0,16},{1,17},{2,18},{3,19},{4,20},{5,21},{6,22},{7,23},{8,24},{9,... | collective-permute-start | bytes 393224 | tf_op jit(solution)/shard_map/ppermute | solution.py:292
  36.4 14.8 %collective-permute-start.33 = (bf16[256,1024]{1,0:T(8,128)(2,1)S(1)}, bf16[256,1024]{1,0:T(8,128)(2,1)S(1)}, u32[]{:S(2)}, u32[]{:S(2)}) collective-permute-start(bf16[256,1024]{1,0:T(8,128)(2,1)S(1)} %convert_element_type.16.refs_4_.refs_11_.refs_6_), channel_id=1, source_target_pairs={{0,4},{1,5},{2,6},{3,7},{4,0},{5,1},{6,2},{7,3},{8,12},{9,13},{10,... | collective-permute-start | bytes 1572872 | tf_op jit(solution)/shard_map/ppermute | solution.py:292
  39.0 23.4 %collective-permute-start.6 = (bf16[256,1024]{1,0:T(8,128)(2,1)S(1)}, bf16[256,1024]{1,0:T(8,128)(2,1)S(1)}, u32[]{:S(2)}, u32[]{:S(2)}) collective-permute-start(bf16[256,1024]{1,0:T(8,128)(2,1)S(1)} %pad_maximum_fusion.refs_0_), channel_id=1, source_target_pairs={{0,4},{1,5},{2,6},{3,7},{4,0},{5,1},{6,2},{7,3},{8,12},{9,13},{10,... | collective-permute-start | bytes 1572872 | tf_op jit(solution)/shard_map/ppermute | solution.py:292
  40.5 34.9 %collective-permute-start.31 = (bf16[256,1024]{1,0:T(8,128)(2,1)S(1)}, bf16[256,1024]{1,0:T(8,128)(2,1)S(1)}, u32[]{:S(2)}, u32[]{:S(2)}) collective-permute-start(bf16[256,1024]{1,0:T(8,128)(2,1)S(1)} %convert_element_type.16.refs_4_.refs_11_.refs_6_), channel_id=1, source_target_pairs={{0,1},{1,0},{2,3},{3,2},{4,5},{5,4},{6,7},{7,6},{8,9},{9,8},{10,11... | collective-permute-start | bytes 1572872 | tf_op jit(solution)/shard_map/ppermute | solution.py:292
  43.2 24.8 %collective-permute-start.34 = (bf16[128,1024]{1,0:T(8,128)(2,1)S(1)}, bf16[128,1024]{1,0:T(8,128)(2,1)S(1)}, u32[]{:S(2)}, u32[]{:S(2)}) collective-permute-start(bf16[128,1024]{1,0:T(8,128)(2,1)S(1)} %slice.23), channel_id=1, source_target_pairs={{0,4},{1,5},{2,6},{3,7},{4,0},{5,1},{6,2},{7,3},{8,12},{9,13},{10,... | collective-permute-start | bytes 786440 | tf_op jit(solution)/shard_map/ppermute | solution.py:292
  48.1 20.0 %collective-permute-start.18 = (bf16[64,1152]{1,0:T(8,128)(2,1)S(1)}, bf16[64,1152]{1,0:T(8,128)(2,1)S(1)}, u32[]{:S(2)}, u32[]{:S(2)}) collective-permute-start(bf16[64,1152]{1,0:T(8,128)(2,1)S(1)} %get-tuple-element.10), channel_id=1, source_target_pairs={{0,24},{1,25},{2,26},{3,27},{4,28},{5,29},{6,30},{7,31},{8,0},{9,1... | collective-permute-start | bytes 442376 | tf_op jit(solution)/shard_map/ppermute | solution.py:292
  51.2 17.5 %collective-permute-start.19 = (bf16[64,1152]{1,0:T(8,128)(2,1)S(1)}, bf16[64,1152]{1,0:T(8,128)(2,1)S(1)}, u32[]{:S(2)}, u32[]{:S(2)}) collective-permute-start(bf16[64,1152]{1,0:T(8,128)(2,1)S(1)} %get-tuple-element.11), channel_id=1, source_target_pairs={{0,16},{1,17},{2,18},{3,19},{4,20},{5,21},{6,22},{7,23},{8,24},{9,... | collective-permute-start | bytes 442376 | tf_op jit(solution)/shard_map/ppermute | solution.py:292
  62.4 13.0 %collective-permute-start.7 = (bf16[128,1024]{1,0:T(8,128)(2,1)S(1)}, bf16[128,1024]{1,0:T(8,128)(2,1)S(1)}, u32[]{:S(2)}, u32[]{:S(2)}) collective-permute-start(bf16[128,1024]{1,0:T(8,128)(2,1)S(1)} %pad_maximum_fusion.1), channel_id=1, source_target_pairs={{0,4},{1,5},{2,6},{3,7},{4,0},{5,1},{6,2},{7,3},{8,12},{9,13},{10,... | collective-permute-start | bytes 786440 | tf_op jit(solution)/shard_map/ppermute | solution.py:292
  68.0 9.2 %collective-permute-start.35 = (bf16[128,1024]{1,0:T(8,128)(2,1)S(1)}, bf16[128,1024]{1,0:T(8,128)(2,1)S(1)}, u32[]{:S(2)}, u32[]{:S(2)}) collective-permute-start(bf16[128,1024]{1,0:T(8,128)(2,1)S(1)} %slice.24), channel_id=1, source_target_pairs={{0,2},{1,3},{2,0},{3,1},{4,6},{5,7},{6,4},{7,5},{8,10},{9,11},{10,... | collective-permute-start | bytes 786440 | tf_op jit(solution)/shard_map/ppermute | solution.py:292
  68.6 12.5 %collective-permute-start.8 = (bf16[128,1024]{1,0:T(8,128)(2,1)S(1)}, bf16[128,1024]{1,0:T(8,128)(2,1)S(1)}, u32[]{:S(2)}, u32[]{:S(2)}) collective-permute-start(bf16[128,1024]{1,0:T(8,128)(2,1)S(1)} %slice.20), channel_id=1, source_target_pairs={{0,2},{1,3},{2,0},{3,1},{4,6},{5,7},{6,4},{7,5},{8,10},{9,11},{10,... | collective-permute-start | bytes 786440 | tf_op jit(solution)/shard_map/ppermute | solution.py:292
  74.9 8.8 %collective-permute-start.38 = (bf16[128,1024]{1,0:T(8,128)(2,1)S(1)}, bf16[128,1024]{1,0:T(8,128)(2,1)S(1)}, u32[]{:S(2)}, u32[]{:S(2)}) collective-permute-start(bf16[128,1024]{1,0:T(8,128)(2,1)S(1)} %collective-permute-done.34.refs_8_), channel_id=1, source_target_pairs={{0,1},{1,0},{2,3},{3,2},{4,5},{5,4},{6,7},{7,6},{8,9},{9,8},{10,11... | collective-permute-start | bytes 786440 | tf_op jit(solution)/shard_map/ppermute | solution.py:292
  75.4 8.4 %collective-permute-start.25 = (bf16[64,1024]{1,0:T(8,128)(2,1)S(1)}, bf16[64,1024]{1,0:T(8,128)(2,1)S(1)}, u32[]{:S(2)}, u32[]{:S(2)}) collective-permute-start(bf16[64,1024]{1,0:T(8,128)(2,1)S(1)} %get-tuple-element.15.refs_0_), channel_id=1, source_target_pairs={{0,8},{1,9},{2,10},{3,11},{4,12},{5,13},{6,14},{7,15},{8,16},{9,17... | collective-permute-start | bytes 393224 | tf_op jit(solution)/shard_map/ppermute | solution.py:292
  75.5 13.0 %collective-permute-start.26 = (bf16[64,1024]{1,0:T(8,128)(2,1)S(1)}, bf16[64,1024]{1,0:T(8,128)(2,1)S(1)}, u32[]{:S(2)}, u32[]{:S(2)}) collective-permute-start(bf16[64,1024]{1,0:T(8,128)(2,1)S(1)} %get-tuple-element.15.refs_0_), channel_id=1, source_target_pairs={{0,16},{1,17},{2,18},{3,19},{4,20},{5,21},{6,22},{7,23},{8,24},{9,... | collective-permute-start | bytes 393224 | tf_op jit(solution)/shard_map/ppermute | solution.py:292
  77.3 12.7 %collective-permute-start.27 = (bf16[64,1024]{1,0:T(8,128)(2,1)S(1)}, bf16[64,1024]{1,0:T(8,128)(2,1)S(1)}, u32[]{:S(2)}, u32[]{:S(2)}) collective-permute-start(bf16[64,1024]{1,0:T(8,128)(2,1)S(1)} %get-tuple-element.15.refs_0_), channel_id=1, source_target_pairs={{0,24},{1,25},{2,26},{3,27},{4,28},{5,29},{6,30},{7,31},{8,0},{9,1... | collective-permute-start | bytes 393224 | tf_op jit(solution)/shard_map/ppermute | solution.py:292
  81.1 19.9 %collective-permute-start.36 = (bf16[256,1024]{1,0:T(8,128)(2,1)S(1)}, bf16[256,1024]{1,0:T(8,128)(2,1)S(1)}, u32[]{:S(2)}, u32[]{:S(2)}) collective-permute-start(bf16[256,1024]{1,0:T(8,128)(2,1)S(1)} %collective-permute-done.32.refs_6_), channel_id=1, source_target_pairs={{0,1},{1,0},{2,3},{3,2},{4,5},{5,4},{6,7},{7,6},{8,9},{9,8},{10,11... | collective-permute-start | bytes 1572872 | tf_op jit(solution)/shard_map/ppermute | solution.py:292
  83.8 17.3 %collective-permute-start.37 = (bf16[256,1024]{1,0:T(8,128)(2,1)S(1)}, bf16[256,1024]{1,0:T(8,128)(2,1)S(1)}, u32[]{:S(2)}, u32[]{:S(2)}) collective-permute-start(bf16[256,1024]{1,0:T(8,128)(2,1)S(1)} %collective-permute-done.33.refs_7_), channel_id=1, source_target_pairs={{0,1},{1,0},{2,3},{3,2},{4,5},{5,4},{6,7},{7,6},{8,9},{9,8},{10,11... | collective-permute-start | bytes 1572872 | tf_op jit(solution)/shard_map/ppermute | solution.py:292
  90.0 7.9 %collective-permute-start.23 = (bf16[64,1152]{1,0:T(8,128)(2,1)S(1)}, bf16[64,1152]{1,0:T(8,128)(2,1)S(1)}, u32[]{:S(2)}, u32[]{:S(2)}) collective-permute-start(bf16[64,1152]{1,0:T(8,128)(2,1)S(1)} %get-tuple-element.14), channel_id=1, source_target_pairs={{0,6},{1,7},{2,4},{3,5},{4,2},{5,3},{6,0},{7,1},{8,14},{9,15},{10,... | collective-permute-start | bytes 442376 | tf_op jit(solution)/shard_map/ppermute | solution.py:292
  90.5 27.3 %collective-permute-start.45 = (bf16[192,1024]{1,0:T(8,128)(2,1)S(1)}, bf16[192,1024]{1,0:T(8,128)(2,1)S(1)}, u32[]{:S(2)}, u32[]{:S(2)}) collective-permute-start(bf16[192,1024]{1,0:T(8,128)(2,1)S(1)} %constant_dynamic-update-slice_fusion), channel_id=1, source_target_pairs={{0,2},{1,3},{2,0},{3,1},{4,6},{5,7},{6,4},{7,5},{8,10},{9,11},{10,... | collective-permute-start | bytes 1179656 | tf_op jit(solution)/shard_map/ppermute | solution.py:292
  95.2 22.6 %collective-permute-start.46 = (bf16[192,1024]{1,0:T(8,128)(2,1)S(1)}, bf16[192,1024]{1,0:T(8,128)(2,1)S(1)}, u32[]{:S(2)}, u32[]{:S(2)}) collective-permute-start(bf16[192,1024]{1,0:T(8,128)(2,1)S(1)} %constant_dynamic-update-slice_fusion), channel_id=1, source_target_pairs={{0,4},{1,5},{2,6},{3,7},{4,0},{5,1},{6,2},{7,3},{8,12},{9,13},{10,... | collective-permute-start | bytes 1179656 | tf_op jit(solution)/shard_map/ppermute | solution.py:292
  100.4 37.8 %collective-permute-start.24 = (f32[256,1152]{1,0:T(8,128)S(1)}, f32[256,1152]{1,0:T(8,128)S(1)}, u32[]{:S(2)}, u32[]{:S(2)}) collective-permute-start(f32[256,1152]{1,0:T(8,128)S(1)} %sums.5), channel_id=1, source_target_pairs={{0,1},{1,0},{2,3},{3,2},{4,5},{5,4},{6,7},{7,6},{8,9},{9,8},{10,11... | collective-permute-start | bytes 3538952 | tf_op jit(solution)/shard_map/ppermute | solution.py:292
  119.2 21.9 %collective-permute-start.49 = (f32[256,1152]{1,0:T(8,128)S(1)}, f32[256,1152]{1,0:T(8,128)S(1)}, u32[]{:S(2)}, u32[]{:S(2)}) collective-permute-start(f32[256,1152]{1,0:T(8,128)S(1)} %sums.8), channel_id=1, source_target_pairs={{0,1},{1,0},{2,3},{3,2},{4,5},{5,4},{6,7},{7,6},{8,9},{9,8},{10,11... | collective-permute-start | bytes 3538952 | tf_op jit(solution)/shard_map/ppermute | solution.py:292
  119.3 12.4 %collective-permute-start.28 = (bf16[192,1024]{1,0:T(8,128)(2,1)S(1)}, bf16[192,1024]{1,0:T(8,128)(2,1)S(1)}, u32[]{:S(2)}, u32[]{:S(2)}) collective-permute-start(bf16[192,1024]{1,0:T(8,128)(2,1)S(1)} %constant_dynamic-update-slice_fusion), channel_id=1, source_target_pairs={{0,6},{1,7},{2,4},{3,5},{4,2},{5,3},{6,0},{7,1},{8,14},{9,15},{10,... | collective-permute-start | bytes 1179656 | tf_op jit(solution)/shard_map/ppermute | solution.py:292
  131.7 9.4 %collective-permute-start.30 = (bf16[192,1024]{1,0:T(8,128)(2,1)S(1)}, bf16[192,1024]{1,0:T(8,128)(2,1)S(1)}, u32[]{:S(2)}, u32[]{:S(2)}) collective-permute-start(bf16[192,1024]{1,0:T(8,128)(2,1)S(1)} %collective-permute-done.28.refs_1_), channel_id=1, source_target_pairs={{0,1},{1,0},{2,3},{3,2},{4,5},{5,4},{6,7},{7,6},{8,9},{9,8},{10,11... | collective-permute-start | bytes 1179656 | tf_op jit(solution)/shard_map/ppermute | solution.py:292
  (22 other events, 141.0 us)

commit v2 on v1

--- a/solution.py
+++ b/solution.py
@@ -362,9 +362,10 @@
 
         stats = stats_of(notes, part)
         stats = [stats] + spread(stats)
-        others = [sums(chunks_two[:-1], stats[:-1], near_two[m]) for m in range(1, lc)]
+        begun = [sums(chunks_two[:1], stats[:1], near_two[m]) for m in range(lc)]
+        others = [sums(chunks_two[1:-1], stats[1:-1], near_two[m], begun[m : m + 1]) for m in range(1, lc)]
         sent = [shift(other, c=-m) for m, other in enumerate(others, 1)]
-        early = sums(chunks_two[:-1], stats[:-1], near_two[0])
+        early = sums(chunks_two[1:-1], stats[1:-1], near_two[0], begun[:1])
         last = [chunks_two[-1][0], chunks_two[-1][1]]
         last = [last] + [[shift(last[0], c=m), shift(last[1], c=m)] for m in range(1, lc)]
         stats = [stats[-1]] + [shift(stats[-1], c=m) for m in range(1, lc)]

time: 143 us -> 142 us (level)
  waiting for transfers between devices: 66.5 us -> 64.9 us
    ppermute x50, waiting for transfers between devices: 66.5 us -> 64.9 us  [shift(): return lax.ppermute(value, axes, pairs)]
    pallas_call x5 -> x7, Pallas kernels: 9.75 us -> 10.2 us  [sums(): pl.pallas_call(functools.partial(sums_kernel, tuple((len(chunk) for chunk...]
  transfers between devices with their start and end apart: 50 -> 50, of which waited for: 21 -> 20; matrix products, arithmetic and copies ran while one was open for 4% -> 4% of each run, Pallas kernels for 10% -> 11%
where the time goes in v2:
time: 142 us
  waiting for transfers between devices  64.9 us (46%)
  starting transfers between devices  51.7 us (36%)
  Pallas kernels  17.3 us (12%)
  other arithmetic  3.45 us (2%)
  local copies, waits for them, and re-layouts  3.04 us (2%)
  between operations  1.59 us (1%)
    ppermute x50, waiting for transfers between devices, shift(): return lax.ppermute(value, axes, pairs)  64.9 us
    ppermute x50, starting transfers between devices, shift(): return lax.ppermute(value, axes, pairs)  51.7 us
    pallas_call x7, Pallas kernels, sums(): pl.pallas_call(functools.partial(sums_kernel, tuple((len(chunk) for chunk...  10.2 us
    pallas_call x2, Pallas kernels, attend(): pl.pallas_call(functools.partial(attend_kernel, len(rows), len(books), re...  6.62 us
  transfers between devices with their start and end apart: 50, of which 20 were waited for; matrix products, arithmetic and copies ran while one was open for 4% of the time, Pallas kernels for 11%

profile of v2, /device:TPU:0, one launch (start us, length us, event | category | flops | bytes accessed | tf_op | source)
XLA Modules:
  0.0 142.0 jit_solution(7595594760965277799)
XLA Ops:
  2.0 3.1 %collective-permute-start.10 = (bf16[256,1024]{1,0:T(8,128)(2,1)S(1)}, bf16[256,1024]{1,0:T(8,128)(2,1)}, u32[]{:S(2)}, u32[]{:S(2)}) collective-permute-start(bf16[256,1024]{1,0:T(8,128)(2,1)S(1)} %convert_element_type.15.refs_4_.refs_12_), channel_id=1, source_target_pairs={{0,2},{1,3},{2,0},{3,1},{4,6},{5,7},{6,4},{7,5},{8,10},{9,11},{10,... | collective-permute-start | bytes 1572872 | tf_op jit(solution)/shard_map/ppermute | solution.py:292
  7.6 1.6 %collective-permute-start = (bf16[64,1024]{1,0:T(8,128)(2,1)S(1)}, bf16[64,1024]{1,0:T(8,128)(2,1)S(1)}, u32[]{:S(2)}, u32[]{:S(2)}) collective-permute-start(bf16[64,1024]{1,0:T(8,128)(2,1)S(1)} %get-tuple-element.16.refs_0_), channel_id=1, source_target_pairs={{0,8},{1,9},{2,10},{3,11},{4,12},{5,13},{6,14},{7,15},{8,16},{9,17... | collective-permute-start | bytes 393224 | tf_op jit(solution)/shard_map/ppermute | solution.py:292
  9.2 2.6 %collective-permute-start.1 = (bf16[64,1024]{1,0:T(8,128)(2,1)S(1)}, bf16[64,1024]{1,0:T(8,128)(2,1)}, u32[]{:S(2)}, u32[]{:S(2)}) collective-permute-start(bf16[64,1024]{1,0:T(8,128)(2,1)S(1)} %get-tuple-element.16.refs_0_), channel_id=1, source_target_pairs={{0,16},{1,17},{2,18},{3,19},{4,20},{5,21},{6,22},{7,23},{8,24},{9,... | collective-permute-start | bytes 393224 | tf_op jit(solution)/shard_map/ppermute | solution.py:292
  11.9 4.0 %collective-permute-done.refs_1_ = bf16[64,1024]{1,0:T(8,128)(2,1)S(1)} collective-permute-done((bf16[64,1024]{1,0:T(8,128)(2,1)S(1)}, bf16[64,1024]{1,0:T(8,128)(2,1)S(1)}, u32[]{:S(2)}, u32[]{:S(2)}) %collective-permute-start) | collective-permute-done | bytes 131104 | tf_op jit(solution)/shard_map/ppermute | solution.py:292
  17.3 1.6 %collective-permute-start.32 = (bf16[256,1024]{1,0:T(8,128)(2,1)S(1)}, bf16[256,1024]{1,0:T(8,128)(2,1)S(1)}, u32[]{:S(2)}, u32[]{:S(2)}) collective-permute-start(bf16[256,1024]{1,0:T(8,128)(2,1)S(1)} %convert_element_type.16.refs_4_.refs_5_.refs_6_), channel_id=1, source_target_pairs={{0,2},{1,3},{2,0},{3,1},{4,6},{5,7},{6,4},{7,5},{8,10},{9,11},{10,... | collective-permute-start | bytes 1572872 | tf_op jit(solution)/shard_map/ppermute | solution.py:292
  24.5 3.1 %collective-permute-start.4 = (bf16[64,1024]{1,0:T(8,128)(2,1)S(1)}, bf16[64,1024]{1,0:T(8,128)(2,1)S(1)}, u32[]{:S(2)}, u32[]{:S(2)}) collective-permute-start(bf16[64,1024]{1,0:T(8,128)(2,1)S(1)} %dynamic-slice_convert_fusion.refs_1_), channel_id=1, source_target_pairs={{0,16},{1,17},{2,18},{3,19},{4,20},{5,21},{6,22},{7,23},{8,24},{9,... | collective-permute-start | bytes 393224 | tf_op jit(solution)/shard_map/ppermute | solution.py:292
  28.7 3.0 %collective-permute-done.3.refs_2_ = bf16[64,1024]{1,0:T(8,128)(2,1)S(1)} collective-permute-done((bf16[64,1024]{1,0:T(8,128)(2,1)S(1)}, bf16[64,1024]{1,0:T(8,128)(2,1)S(1)}, u32[]{:S(2)}, u32[]{:S(2)}) %collective-permute-start.3) | collective-permute-done | bytes 131104 | tf_op jit(solution)/shard_map/ppermute | solution.py:292
  32.1 3.6 %collective-permute-done.4.refs_3_ = bf16[64,1024]{1,0:T(8,128)(2,1)S(1)} collective-permute-done((bf16[64,1024]{1,0:T(8,128)(2,1)S(1)}, bf16[64,1024]{1,0:T(8,128)(2,1)S(1)}, u32[]{:S(2)}, u32[]{:S(2)}) %collective-permute-start.4) | collective-permute-done | bytes 131104 | tf_op jit(solution)/shard_map/ppermute | solution.py:292
  40.8 2.3 %collective-permute-start.5 = (bf16[64,1024]{1,0:T(8,128)(2,1)S(1)}, bf16[64,1024]{1,0:T(8,128)(2,1)S(1)}, u32[]{:S(2)}, u32[]{:S(2)}) collective-permute-start(bf16[64,1024]{1,0:T(8,128)(2,1)S(1)} %dynamic-slice_convert_fusion.refs_1_), channel_id=1, source_target_pairs={{0,24},{1,25},{2,26},{3,27},{4,28},{5,29},{6,30},{7,31},{8,0},{9,1... | collective-permute-start | bytes 393224 | tf_op jit(solution)/shard_map/ppermute | solution.py:292
  43.5 4.5 %attend.1 = (bf16[64,1152]{1,0:T(8,128)(2,1)S(1)}, bf16[64,1152]{1,0:T(8,128)(2,1)S(1)}, bf16[64,1152]{1,0:T(8,128)(2,1)S(1)}, bf16[64,1152]{1,0:T(8,128)(2,1)S(1)}) custom-call(bf16[64,1024]{1,0:T(8,128)(2,1)S(1)} %get-tuple-element.16.refs_0_, bf16[64,1024]{1,0:T(8,128)(2,1)S(1)} %copy-done.3, bf16[64,1024]{1,0:T(8,128)(2,1)} %collective-permute-done.1.refs_2_, ...), custom_call_target="tpu_custom_call" | custom-call | flops 2147483648 | bytes 4718592 | tf_op jit(solution)/shard_map/attend/pallas_call | solution.py:117
  48.0 2.6 %collective-permute-start.18 = (bf16[64,1152]{1,0:T(8,128)(2,1)S(1)}, bf16[64,1152]{1,0:T(8,128)(2,1)S(1)}, u32[]{:S(2)}, u32[]{:S(2)}) collective-permute-start(bf16[64,1152]{1,0:T(8,128)(2,1)S(1)} %get-tuple-element.10), channel_id=1, source_target_pairs={{0,24},{1,25},{2,26},{3,27},{4,28},{5,29},{6,30},{7,31},{8,0},{9,1... | collective-permute-start | bytes 442376 | tf_op jit(solution)/shard_map/ppermute | solution.py:292
  51.2 11.2 %collective-permute-done.6.refs_5_ = bf16[256,1024]{1,0:T(8,128)(2,1)S(1)} collective-permute-done((bf16[256,1024]{1,0:T(8,128)(2,1)S(1)}, bf16[256,1024]{1,0:T(8,128)(2,1)S(1)}, u32[]{:S(2)}, u32[]{:S(2)}) %collective-permute-start.6) | collective-permute-done | bytes 524320 | tf_op jit(solution)/shard_map/ppermute | solution.py:292
  63.9 4.1 %collective-permute-done.34.refs_8_ = bf16[128,1024]{1,0:T(8,128)(2,1)S(1)} collective-permute-done((bf16[128,1024]{1,0:T(8,128)(2,1)S(1)}, bf16[128,1024]{1,0:T(8,128)(2,1)S(1)}, u32[]{:S(2)}, u32[]{:S(2)}) %collective-permute-start.34) | collective-permute-done | bytes 262176 | tf_op jit(solution)/shard_map/ppermute | solution.py:292
  68.6 1.6 %collective-permute-start.8 = (bf16[128,1024]{1,0:T(8,128)(2,1)S(1)}, bf16[128,1024]{1,0:T(8,128)(2,1)S(1)}, u32[]{:S(2)}, u32[]{:S(2)}) collective-permute-start(bf16[128,1024]{1,0:T(8,128)(2,1)S(1)} %slice.20), channel_id=1, source_target_pairs={{0,2},{1,3},{2,0},{3,1},{4,6},{5,7},{6,4},{7,5},{8,10},{9,11},{10,... | collective-permute-start | bytes 786440 | tf_op jit(solution)/shard_map/ppermute | solution.py:292
  70.2 4.7 %collective-permute-done.20.refs_4_ = bf16[64,1152]{1,0:T(8,128)(2,1)S(1)} collective-permute-done((bf16[64,1152]{1,0:T(8,128)(2,1)S(1)}, bf16[64,1152]{1,0:T(8,128)(2,1)S(1)}, u32[]{:S(2)}, u32[]{:S(2)}) %collective-permute-start.20) | collective-permute-done | bytes 147488 | tf_op jit(solution)/shard_map/ppermute | solution.py:292
  75.6 1.7 %collective-permute-done.35.refs_9_ = bf16[128,1024]{1,0:T(8,128)(2,1)S(1)} collective-permute-done((bf16[128,1024]{1,0:T(8,128)(2,1)S(1)}, bf16[128,1024]{1,0:T(8,128)(2,1)S(1)}, u32[]{:S(2)}, u32[]{:S(2)}) %collective-permute-start.35) | collective-permute-done | bytes 262176 | tf_op jit(solution)/shard_map/ppermute | solution.py:292
  77.3 3.8 %collective-permute-start.27 = (bf16[64,1024]{1,0:T(8,128)(2,1)S(1)}, bf16[64,1024]{1,0:T(8,128)(2,1)S(1)}, u32[]{:S(2)}, u32[]{:S(2)}) collective-permute-start(bf16[64,1024]{1,0:T(8,128)(2,1)S(1)} %get-tuple-element.15.refs_0_), channel_id=1, source_target_pairs={{0,24},{1,25},{2,26},{3,27},{4,28},{5,29},{6,30},{7,31},{8,0},{9,1... | collective-permute-start | bytes 393224 | tf_op jit(solution)/shard_map/ppermute | solution.py:292
  81.1 2.6 %collective-permute-done.25.refs_1_ = bf16[64,1024]{1,0:T(8,128)(2,1)S(1)} collective-permute-done((bf16[64,1024]{1,0:T(8,128)(2,1)S(1)}, bf16[64,1024]{1,0:T(8,128)(2,1)S(1)}, u32[]{:S(2)}, u32[]{:S(2)}) %collective-permute-start.25) | collective-permute-done | bytes 131104 | tf_op jit(solution)/shard_map/ppermute | solution.py:292
  84.4 4.1 %collective-permute-done.26.refs_2_ = bf16[64,1024]{1,0:T(8,128)(2,1)S(1)} collective-permute-done((bf16[64,1024]{1,0:T(8,128)(2,1)S(1)}, bf16[64,1024]{1,0:T(8,128)(2,1)S(1)}, u32[]{:S(2)}, u32[]{:S(2)}) %collective-permute-start.26) | collective-permute-done | bytes 131104 | tf_op jit(solution)/shard_map/ppermute | solution.py:292
  90.5 1.6 %collective-permute-start.45 = (bf16[192,1024]{1,0:T(8,128)(2,1)S(1)}, bf16[192,1024]{1,0:T(8,128)(2,1)S(1)}, u32[]{:S(2)}, u32[]{:S(2)}) collective-permute-start(bf16[192,1024]{1,0:T(8,128)(2,1)S(1)} %constant_dynamic-update-slice_fusion), channel_id=1, source_target_pairs={{0,2},{1,3},{2,0},{3,1},{4,6},{5,7},{6,4},{7,5},{8,10},{9,11},{10,... | collective-permute-start | bytes 1179656 | tf_op jit(solution)/shard_map/ppermute | solution.py:292
  92.1 3.1 %collective-permute-done.22.refs_10_.refs_2_ = bf16[64,1152]{1,0:T(8,128)(2,1)S(1)} collective-permute-done((bf16[64,1152]{1,0:T(8,128)(2,1)S(1)}, bf16[64,1152]{1,0:T(8,128)(2,1)S(1)}, u32[]{:S(2)}, u32[]{:S(2)}) %collective-permute-start.22) | collective-permute-done | bytes 147488 | tf_op jit(solution)/shard_map/ppermute | solution.py:292
  98.6 1.9 %sums.7 = f32[256,1152]{1,0:T(8,128)S(1)} custom-call(bf16[256,1024]{1,0:T(8,128)(2,1)S(1)} %pad_maximum_fusion.refs_0_, bf16[64,1024]{1,0:T(8,128)(2,1)S(1)} %dynamic-slice_convert_fusion.refs_1_, bf16[64,1024]{1,0:T(8,128)(2,1)S(1)} %collective-permute-done.3.refs_2_, bf16[64,1024]{1,0:T(8,128)(2,1)S(1)} %collective-permute-done.4.refs_3_, ...), custom_call_target="tpu_custom_call" | custom-call | flops 1073741824 | bytes 3670016 | tf_op jit(solution)/shard_map/sums/pallas_call | solution.py:260
  101.0 2.1 %levels.1.refs_0_ = f32[1,320]{1,0:T(1,128)S(1)} custom-call(bf16[64,1024]{1,0:T(8,128)(2,1)S(1)} %get-tuple-element.15.refs_0_, bf16[64,1024]{1,0:T(8,128)(2,1)S(1)} %collective-permute-done.25.refs_1_, bf16[64,1024]{1,0:T(8,128)(2,1)S(1)} %collective-permute-done.26.refs_2_, bf16[64,1024]{1,0:T(8,128)(2,1)S(1)} %collective-permute-done.27.refs_3_, ...), custom_call_target="tpu_custom_call" | custom-call | flops 1073741824 | bytes 4718592 | tf_op jit(solution)/shard_map/levels/pallas_call | solution.py:117
  104.2 2.4 %collective-permute-start.41 = (f32[1,320]{1,0:T(1,128)S(1)}, f32[1,320]{1,0:T(1,128)S(1)}, u32[]{:S(2)}, u32[]{:S(2)}) collective-permute-start(f32[1,320]{1,0:T(1,128)S(1)} %levels.1.refs_0_), channel_id=1, source_target_pairs={{0,16},{1,17},{2,18},{3,19},{4,20},{5,21},{6,22},{7,23},{8,24},{9,... | collective-permute-start | bytes 3848 | tf_op jit(solution)/shard_map/ppermute | solution.py:292
  106.7 1.8 %collective-permute-done.40.refs_1_ = f32[1,320]{1,0:T(1,128)S(1)} collective-permute-done((f32[1,320]{1,0:T(1,128)S(1)}, f32[1,320]{1,0:T(1,128)S(1)}, u32[]{:S(2)}, u32[]{:S(2)}) %collective-permute-start.40) | collective-permute-done | bytes 1312 | tf_op jit(solution)/shard_map/ppermute | solution.py:292
  109.7 2.4 %collective-permute-done.42.refs_3_ = f32[1,320]{1,0:T(1,128)S(1)} collective-permute-done((f32[1,320]{1,0:T(1,128)S(1)}, f32[1,320]{1,0:T(1,128)S(1)}, u32[]{:S(2)}, u32[]{:S(2)}) %collective-permute-start.42) | collective-permute-done | bytes 1312 | tf_op jit(solution)/shard_map/ppermute | solution.py:292
  112.2 2.0 %collective-permute-start.47 = (f32[1,256]{1,0:T(1,128)S(1)}, f32[1,256]{1,0:T(1,128)S(1)}, u32[]{:S(2)}, u32[]{:S(2)}) collective-permute-start(f32[1,256]{1,0:T(1,128)S(1)} %stats.1.refs_4_), channel_id=1, source_target_pairs={{0,2},{1,3},{2,0},{3,1},{4,6},{5,7},{6,4},{7,5},{8,10},{9,11},{10,... | collective-permute-start | bytes 3080 | tf_op jit(solution)/shard_map/ppermute | solution.py:292
  114.2 1.5 %collective-permute-start.48 = (f32[1,256]{1,0:T(1,128)S(1)}, f32[1,256]{1,0:T(1,128)S(1)}, u32[]{:S(2)}, u32[]{:S(2)}) collective-permute-start(f32[1,256]{1,0:T(1,128)S(1)} %stats.1.refs_4_), channel_id=1, source_target_pairs={{0,4},{1,5},{2,6},{3,7},{4,0},{5,1},{6,2},{7,3},{8,12},{9,13},{10,... | collective-permute-start | bytes 3080 | tf_op jit(solution)/shard_map/ppermute | solution.py:292
  120.2 10.9 %collective-permute-done.28.refs_1_ = bf16[192,1024]{1,0:T(8,128)(2,1)S(1)} collective-permute-done((bf16[192,1024]{1,0:T(8,128)(2,1)S(1)}, bf16[192,1024]{1,0:T(8,128)(2,1)S(1)}, u32[]{:S(2)}, u32[]{:S(2)}) %collective-permute-start.28) | collective-permute-done | bytes 393248 | tf_op jit(solution)/shard_map/ppermute | solution.py:292
  133.4 2.3 %collective-permute-done.43.refs_4_ = f32[1,256]{1,0:T(1,128)S(1)} collective-permute-done((f32[1,256]{1,0:T(1,128)S(1)}, f32[1,256]{1,0:T(1,128)S(1)}, u32[]{:S(2)}, u32[]{:S(2)}) %collective-permute-start.43) | collective-permute-done | bytes 1056 | tf_op jit(solution)/shard_map/ppermute | solution.py:292
  137.1 2.9 %sums.8 = f32[256,1024]{1,0:T(8,128)} custom-call(bf16[256,1024]{1,0:T(8,128)(2,1)S(1)} %pad_maximum_fusion.refs_0_, bf16[64,1024]{1,0:T(8,128)(2,1)S(1)} %dynamic-slice_convert_fusion.refs_1_, bf16[64,1024]{1,0:T(8,128)(2,1)S(1)} %collective-permute-done.3.refs_2_, bf16[64,1024]{1,0:T(8,128)(2,1)S(1)} %collective-permute-done.4.refs_3_, ...), custom_call_target="tpu_custom_call" | custom-call | flops 1073741824 | bytes 3670016 | tf_op jit(solution)/shard_map/sums/pallas_call | solution.py:260
  140.1 2.0 %sums.13 = f32[256,1024]{1,0:T(8,128)} custom-call(bf16[64,1152]{1,0:T(8,128)(2,1)S(1)} %collective-permute-done.23.refs_11_.refs_0_, bf16[192,1024]{1,0:T(8,128)(2,1)S(1)} %collective-permute-done.28.refs_1_, bf16[64,1152]{1,0:T(8,128)(2,1)S(1)} %collective-permute-done.29.refs_2_, bf16[192,1024]{1,0:T(8,128)(2,1)S(1)} %collective-permute-done.30.refs_3_, ...), custom_call_target="tpu_custom_call" | custom-call | flops 536870912 | bytes 2621440 | tf_op jit(solution)/shard_map/sums/pallas_call | solution.py:260
  (102 shorter events, 37.5 us)
Async XLA Ops:
  2.0 15.3 %collective-permute-start.10 = (bf16[256,1024]{1,0:T(8,128)(2,1)S(1)}, bf16[256,1024]{1,0:T(8,128)(2,1)}, u32[]{:S(2)}, u32[]{:S(2)}) collective-permute-start(bf16[256,1024]{1,0:T(8,128)(2,1)S(1)} %convert_element_type.15.refs_4_.refs_12_), channel_id=1, source_target_pairs={{0,2},{1,3},{2,0},{3,1},{4,6},{5,7},{6,4},{7,5},{8,10},{9,11},{10,... | collective-permute-start | bytes 1572872 | tf_op jit(solution)/shard_map/ppermute | solution.py:292
  5.1 19.4 %collective-permute-start.11 = (bf16[256,1024]{1,0:T(8,128)(2,1)S(1)}, bf16[256,1024]{1,0:T(8,128)(2,1)}, u32[]{:S(2)}, u32[]{:S(2)}) collective-permute-start(bf16[256,1024]{1,0:T(8,128)(2,1)S(1)} %convert_element_type.15.refs_4_.refs_12_), channel_id=1, source_target_pairs={{0,4},{1,5},{2,6},{3,7},{4,0},{5,1},{6,2},{7,3},{8,12},{9,13},{10,... | collective-permute-start | bytes 1572872 | tf_op jit(solution)/shard_map/ppermute | solution.py:292
  6.6 29.2 %collective-permute-start.9 = (bf16[256,1024]{1,0:T(8,128)(2,1)S(1)}, bf16[256,1024]{1,0:T(8,128)(2,1)S(1)}, u32[]{:S(2)}, u32[]{:S(2)}) collective-permute-start(bf16[256,1024]{1,0:T(8,128)(2,1)S(1)} %convert_element_type.15.refs_4_.refs_12_), channel_id=1, source_target_pairs={{0,1},{1,0},{2,3},{3,2},{4,5},{5,4},{6,7},{7,6},{8,9},{9,8},{10,11... | collective-permute-start | bytes 1572872 | tf_op jit(solution)/shard_map/ppermute | solution.py:292
  7.6 8.3 %collective-permute-start = (bf16[64,1024]{1,0:T(8,128)(2,1)S(1)}, bf16[64,1024]{1,0:T(8,128)(2,1)S(1)}, u32[]{:S(2)}, u32[]{:S(2)}) collective-permute-start(bf16[64,1024]{1,0:T(8,128)(2,1)S(1)} %get-tuple-element.16.refs_0_), channel_id=1, source_target_pairs={{0,8},{1,9},{2,10},{3,11},{4,12},{5,13},{6,14},{7,15},{8,16},{9,17... | collective-permute-start | bytes 393224 | tf_op jit(solution)/shard_map/ppermute | solution.py:292
  9.2 12.0 %collective-permute-start.1 = (bf16[64,1024]{1,0:T(8,128)(2,1)S(1)}, bf16[64,1024]{1,0:T(8,128)(2,1)}, u32[]{:S(2)}, u32[]{:S(2)}) collective-permute-start(bf16[64,1024]{1,0:T(8,128)(2,1)S(1)} %get-tuple-element.16.refs_0_), channel_id=1, source_target_pairs={{0,16},{1,17},{2,18},{3,19},{4,20},{5,21},{6,22},{7,23},{8,24},{9,... | collective-permute-start | bytes 393224 | tf_op jit(solution)/shard_map/ppermute | solution.py:292
  15.9 7.5 %collective-permute-start.2 = (bf16[64,1024]{1,0:T(8,128)(2,1)S(1)}, bf16[64,1024]{1,0:T(8,128)(2,1)}, u32[]{:S(2)}, u32[]{:S(2)}) collective-permute-start(bf16[64,1024]{1,0:T(8,128)(2,1)S(1)} %get-tuple-element.16.refs_0_), channel_id=1, source_target_pairs={{0,24},{1,25},{2,26},{3,27},{4,28},{5,29},{6,30},{7,31},{8,0},{9,1... | collective-permute-start | bytes 393224 | tf_op jit(solution)/shard_map/ppermute | solution.py:292
  17.3 19.1 %collective-permute-start.32 = (bf16[256,1024]{1,0:T(8,128)(2,1)S(1)}, bf16[256,1024]{1,0:T(8,128)(2,1)S(1)}, u32[]{:S(2)}, u32[]{:S(2)}) collective-permute-start(bf16[256,1024]{1,0:T(8,128)(2,1)S(1)} %convert_element_type.16.refs_4_.refs_5_.refs_6_), channel_id=1, source_target_pairs={{0,2},{1,3},{2,0},{3,1},{4,6},{5,7},{6,4},{7,5},{8,10},{9,11},{10,... | collective-permute-start | bytes 1572872 | tf_op jit(solution)/shard_map/ppermute | solution.py:292
  21.2 15.1 %collective-permute-start.12 = (bf16[128,1024]{1,0:T(8,128)(2,1)S(1)}, bf16[128,1024]{1,0:T(8,128)(2,1)S(1)}, u32[]{:S(2)}, u32[]{:S(2)}) collective-permute-start(bf16[128,1024]{1,0:T(8,128)(2,1)S(1)} %slice.21), channel_id=1, source_target_pairs={{0,4},{1,5},{2,6},{3,7},{4,0},{5,1},{6,2},{7,3},{8,12},{9,13},{10,... | collective-permute-start | bytes 786440 | tf_op jit(solution)/shard_map/ppermute | solution.py:292
  23.4 8.3 %collective-permute-start.3 = (bf16[64,1024]{1,0:T(8,128)(2,1)S(1)}, bf16[64,1024]{1,0:T(8,128)(2,1)S(1)}, u32[]{:S(2)}, u32[]{:S(2)}) collective-permute-start(bf16[64,1024]{1,0:T(8,128)(2,1)S(1)} %dynamic-slice_convert_fusion.refs_1_), channel_id=1, source_target_pairs={{0,8},{1,9},{2,10},{3,11},{4,12},{5,13},{6,14},{7,15},{8,16},{9,17... | collective-permute-start | bytes 393224 | tf_op jit(solution)/shard_map/ppermute | solution.py:292
  24.5 11.2 %collective-permute-start.4 = (bf16[64,1024]{1,0:T(8,128)(2,1)S(1)}, bf16[64,1024]{1,0:T(8,128)(2,1)S(1)}, u32[]{:S(2)}, u32[]{:S(2)}) collective-permute-start(bf16[64,1024]{1,0:T(8,128)(2,1)S(1)} %dynamic-slice_convert_fusion.refs_1_), channel_id=1, source_target_pairs={{0,16},{1,17},{2,18},{3,19},{4,20},{5,21},{6,22},{7,23},{8,24},{9,... | collective-permute-start | bytes 393224 | tf_op jit(solution)/shard_map/ppermute | solution.py:292
  36.4 14.8 %collective-permute-start.33 = (bf16[256,1024]{1,0:T(8,128)(2,1)S(1)}, bf16[256,1024]{1,0:T(8,128)(2,1)S(1)}, u32[]{:S(2)}, u32[]{:S(2)}) collective-permute-start(bf16[256,1024]{1,0:T(8,128)(2,1)S(1)} %convert_element_type.16.refs_4_.refs_5_.refs_6_), channel_id=1, source_target_pairs={{0,4},{1,5},{2,6},{3,7},{4,0},{5,1},{6,2},{7,3},{8,12},{9,13},{10,... | collective-permute-start | bytes 1572872 | tf_op jit(solution)/shard_map/ppermute | solution.py:292
  39.0 23.4 %collective-permute-start.6 = (bf16[256,1024]{1,0:T(8,128)(2,1)S(1)}, bf16[256,1024]{1,0:T(8,128)(2,1)S(1)}, u32[]{:S(2)}, u32[]{:S(2)}) collective-permute-start(bf16[256,1024]{1,0:T(8,128)(2,1)S(1)} %pad_maximum_fusion.refs_0_), channel_id=1, source_target_pairs={{0,4},{1,5},{2,6},{3,7},{4,0},{5,1},{6,2},{7,3},{8,12},{9,13},{10,... | collective-permute-start | bytes 1572872 | tf_op jit(solution)/shard_map/ppermute | solution.py:292
  40.5 34.9 %collective-permute-start.31 = (bf16[256,1024]{1,0:T(8,128)(2,1)S(1)}, bf16[256,1024]{1,0:T(8,128)(2,1)S(1)}, u32[]{:S(2)}, u32[]{:S(2)}) collective-permute-start(bf16[256,1024]{1,0:T(8,128)(2,1)S(1)} %convert_element_type.16.refs_4_.refs_5_.refs_6_), channel_id=1, source_target_pairs={{0,1},{1,0},{2,3},{3,2},{4,5},{5,4},{6,7},{7,6},{8,9},{9,8},{10,11... | collective-permute-start | bytes 1572872 | tf_op jit(solution)/shard_map/ppermute | solution.py:292
  43.2 24.8 %collective-permute-start.34 = (bf16[128,1024]{1,0:T(8,128)(2,1)S(1)}, bf16[128,1024]{1,0:T(8,128)(2,1)S(1)}, u32[]{:S(2)}, u32[]{:S(2)}) collective-permute-start(bf16[128,1024]{1,0:T(8,128)(2,1)S(1)} %slice.23), channel_id=1, source_target_pairs={{0,4},{1,5},{2,6},{3,7},{4,0},{5,1},{6,2},{7,3},{8,12},{9,13},{10,... | collective-permute-start | bytes 786440 | tf_op jit(solution)/shard_map/ppermute | solution.py:292
  48.0 20.0 %collective-permute-start.18 = (bf16[64,1152]{1,0:T(8,128)(2,1)S(1)}, bf16[64,1152]{1,0:T(8,128)(2,1)S(1)}, u32[]{:S(2)}, u32[]{:S(2)}) collective-permute-start(bf16[64,1152]{1,0:T(8,128)(2,1)S(1)} %get-tuple-element.10), channel_id=1, source_target_pairs={{0,24},{1,25},{2,26},{3,27},{4,28},{5,29},{6,30},{7,31},{8,0},{9,1... | collective-permute-start | bytes 442376 | tf_op jit(solution)/shard_map/ppermute | solution.py:292
  51.2 17.5 %collective-permute-start.19 = (bf16[64,1152]{1,0:T(8,128)(2,1)S(1)}, bf16[64,1152]{1,0:T(8,128)(2,1)S(1)}, u32[]{:S(2)}, u32[]{:S(2)}) collective-permute-start(bf16[64,1152]{1,0:T(8,128)(2,1)S(1)} %get-tuple-element.11), channel_id=1, source_target_pairs={{0,16},{1,17},{2,18},{3,19},{4,20},{5,21},{6,22},{7,23},{8,24},{9,... | collective-permute-start | bytes 442376 | tf_op jit(solution)/shard_map/ppermute | solution.py:292
  62.4 13.0 %collective-permute-start.7 = (bf16[128,1024]{1,0:T(8,128)(2,1)S(1)}, bf16[128,1024]{1,0:T(8,128)(2,1)S(1)}, u32[]{:S(2)}, u32[]{:S(2)}) collective-permute-start(bf16[128,1024]{1,0:T(8,128)(2,1)S(1)} %pad_maximum_fusion.1), channel_id=1, source_target_pairs={{0,4},{1,5},{2,6},{3,7},{4,0},{5,1},{6,2},{7,3},{8,12},{9,13},{10,... | collective-permute-start | bytes 786440 | tf_op jit(solution)/shard_map/ppermute | solution.py:292
  68.0 9.2 %collective-permute-start.35 = (bf16[128,1024]{1,0:T(8,128)(2,1)S(1)}, bf16[128,1024]{1,0:T(8,128)(2,1)S(1)}, u32[]{:S(2)}, u32[]{:S(2)}) collective-permute-start(bf16[128,1024]{1,0:T(8,128)(2,1)S(1)} %slice.24), channel_id=1, source_target_pairs={{0,2},{1,3},{2,0},{3,1},{4,6},{5,7},{6,4},{7,5},{8,10},{9,11},{10,... | collective-permute-start | bytes 786440 | tf_op jit(solution)/shard_map/ppermute | solution.py:292
  68.6 12.5 %collective-permute-start.8 = (bf16[128,1024]{1,0:T(8,128)(2,1)S(1)}, bf16[128,1024]{1,0:T(8,128)(2,1)S(1)}, u32[]{:S(2)}, u32[]{:S(2)}) collective-permute-start(bf16[128,1024]{1,0:T(8,128)(2,1)S(1)} %slice.20), channel_id=1, source_target_pairs={{0,2},{1,3},{2,0},{3,1},{4,6},{5,7},{6,4},{7,5},{8,10},{9,11},{10,... | collective-permute-start | bytes 786440 | tf_op jit(solution)/shard_map/ppermute | solution.py:292
  74.9 8.8 %collective-permute-start.38 = (bf16[128,1024]{1,0:T(8,128)(2,1)S(1)}, bf16[128,1024]{1,0:T(8,128)(2,1)S(1)}, u32[]{:S(2)}, u32[]{:S(2)}) collective-permute-start(bf16[128,1024]{1,0:T(8,128)(2,1)S(1)} %collective-permute-done.34.refs_8_), channel_id=1, source_target_pairs={{0,1},{1,0},{2,3},{3,2},{4,5},{5,4},{6,7},{7,6},{8,9},{9,8},{10,11... | collective-permute-start | bytes 786440 | tf_op jit(solution)/shard_map/ppermute | solution.py:292
  75.4 8.4 %collective-permute-start.25 = (bf16[64,1024]{1,0:T(8,128)(2,1)S(1)}, bf16[64,1024]{1,0:T(8,128)(2,1)S(1)}, u32[]{:S(2)}, u32[]{:S(2)}) collective-permute-start(bf16[64,1024]{1,0:T(8,128)(2,1)S(1)} %get-tuple-element.15.refs_0_), channel_id=1, source_target_pairs={{0,8},{1,9},{2,10},{3,11},{4,12},{5,13},{6,14},{7,15},{8,16},{9,17... | collective-permute-start | bytes 393224 | tf_op jit(solution)/shard_map/ppermute | solution.py:292
  75.5 13.0 %collective-permute-start.26 = (bf16[64,1024]{1,0:T(8,128)(2,1)S(1)}, bf16[64,1024]{1,0:T(8,128)(2,1)S(1)}, u32[]{:S(2)}, u32[]{:S(2)}) collective-permute-start(bf16[64,1024]{1,0:T(8,128)(2,1)S(1)} %get-tuple-element.15.refs_0_), channel_id=1, source_target_pairs={{0,16},{1,17},{2,18},{3,19},{4,20},{5,21},{6,22},{7,23},{8,24},{9,... | collective-permute-start | bytes 393224 | tf_op jit(solution)/shard_map/ppermute | solution.py:292
  77.3 12.7 %collective-permute-start.27 = (bf16[64,1024]{1,0:T(8,128)(2,1)S(1)}, bf16[64,1024]{1,0:T(8,128)(2,1)S(1)}, u32[]{:S(2)}, u32[]{:S(2)}) collective-permute-start(bf16[64,1024]{1,0:T(8,128)(2,1)S(1)} %get-tuple-element.15.refs_0_), channel_id=1, source_target_pairs={{0,24},{1,25},{2,26},{3,27},{4,28},{5,29},{6,30},{7,31},{8,0},{9,1... | collective-permute-start | bytes 393224 | tf_op jit(solution)/shard_map/ppermute | solution.py:292
  81.1 19.9 %collective-permute-start.36 = (bf16[256,1024]{1,0:T(8,128)(2,1)S(1)}, bf16[256,1024]{1,0:T(8,128)(2,1)S(1)}, u32[]{:S(2)}, u32[]{:S(2)}) collective-permute-start(bf16[256,1024]{1,0:T(8,128)(2,1)S(1)} %collective-permute-done.32.refs_6_), channel_id=1, source_target_pairs={{0,1},{1,0},{2,3},{3,2},{4,5},{5,4},{6,7},{7,6},{8,9},{9,8},{10,11... | collective-permute-start | bytes 1572872 | tf_op jit(solution)/shard_map/ppermute | solution.py:292
  83.8 17.3 %collective-permute-start.37 = (bf16[256,1024]{1,0:T(8,128)(2,1)S(1)}, bf16[256,1024]{1,0:T(8,128)(2,1)S(1)}, u32[]{:S(2)}, u32[]{:S(2)}) collective-permute-start(bf16[256,1024]{1,0:T(8,128)(2,1)S(1)} %collective-permute-done.33.refs_7_), channel_id=1, source_target_pairs={{0,1},{1,0},{2,3},{3,2},{4,5},{5,4},{6,7},{7,6},{8,9},{9,8},{10,11... | collective-permute-start | bytes 1572872 | tf_op jit(solution)/shard_map/ppermute | solution.py:292
  90.0 7.9 %collective-permute-start.23 = (bf16[64,1152]{1,0:T(8,128)(2,1)S(1)}, bf16[64,1152]{1,0:T(8,128)(2,1)S(1)}, u32[]{:S(2)}, u32[]{:S(2)}) collective-permute-start(bf16[64,1152]{1,0:T(8,128)(2,1)S(1)} %get-tuple-element.14), channel_id=1, source_target_pairs={{0,6},{1,7},{2,4},{3,5},{4,2},{5,3},{6,0},{7,1},{8,14},{9,15},{10,... | collective-permute-start | bytes 442376 | tf_op jit(solution)/shard_map/ppermute | solution.py:292
  90.5 27.3 %collective-permute-start.45 = (bf16[192,1024]{1,0:T(8,128)(2,1)S(1)}, bf16[192,1024]{1,0:T(8,128)(2,1)S(1)}, u32[]{:S(2)}, u32[]{:S(2)}) collective-permute-start(bf16[192,1024]{1,0:T(8,128)(2,1)S(1)} %constant_dynamic-update-slice_fusion), channel_id=1, source_target_pairs={{0,2},{1,3},{2,0},{3,1},{4,6},{5,7},{6,4},{7,5},{8,10},{9,11},{10,... | collective-permute-start | bytes 1179656 | tf_op jit(solution)/shard_map/ppermute | solution.py:292
  95.2 22.6 %collective-permute-start.46 = (bf16[192,1024]{1,0:T(8,128)(2,1)S(1)}, bf16[192,1024]{1,0:T(8,128)(2,1)S(1)}, u32[]{:S(2)}, u32[]{:S(2)}) collective-permute-start(bf16[192,1024]{1,0:T(8,128)(2,1)S(1)} %constant_dynamic-update-slice_fusion), channel_id=1, source_target_pairs={{0,4},{1,5},{2,6},{3,7},{4,0},{5,1},{6,2},{7,3},{8,12},{9,13},{10,... | collective-permute-start | bytes 1179656 | tf_op jit(solution)/shard_map/ppermute | solution.py:292
  100.4 36.7 %collective-permute-start.24 = (f32[256,1152]{1,0:T(8,128)S(1)}, f32[256,1152]{1,0:T(8,128)S(1)}, u32[]{:S(2)}, u32[]{:S(2)}) collective-permute-start(f32[256,1152]{1,0:T(8,128)S(1)} %sums.7), channel_id=1, source_target_pairs={{0,1},{1,0},{2,3},{3,2},{4,5},{5,4},{6,7},{7,6},{8,9},{9,8},{10,11... | collective-permute-start | bytes 3538952 | tf_op jit(solution)/shard_map/ppermute | solution.py:292
  118.7 21.4 %collective-permute-start.49 = (f32[256,1152]{1,0:T(8,128)S(1)}, f32[256,1152]{1,0:T(8,128)S(1)}, u32[]{:S(2)}, u32[]{:S(2)}) collective-permute-start(f32[256,1152]{1,0:T(8,128)S(1)} %sums.12), channel_id=1, source_target_pairs={{0,1},{1,0},{2,3},{3,2},{4,5},{5,4},{6,7},{7,6},{8,9},{9,8},{10,11... | collective-permute-start | bytes 3538952 | tf_op jit(solution)/shard_map/ppermute | solution.py:292
  118.8 12.4 %collective-permute-start.28 = (bf16[192,1024]{1,0:T(8,128)(2,1)S(1)}, bf16[192,1024]{1,0:T(8,128)(2,1)S(1)}, u32[]{:S(2)}, u32[]{:S(2)}) collective-permute-start(bf16[192,1024]{1,0:T(8,128)(2,1)S(1)} %constant_dynamic-update-slice_fusion), channel_id=1, source_target_pairs={{0,6},{1,7},{2,4},{3,5},{4,2},{5,3},{6,0},{7,1},{8,14},{9,15},{10,... | collective-permute-start | bytes 1179656 | tf_op jit(solution)/shard_map/ppermute | solution.py:292
  131.2 8.9 %collective-permute-start.30 = (bf16[192,1024]{1,0:T(8,128)(2,1)S(1)}, bf16[192,1024]{1,0:T(8,128)(2,1)S(1)}, u32[]{:S(2)}, u32[]{:S(2)}) collective-permute-start(bf16[192,1024]{1,0:T(8,128)(2,1)S(1)} %collective-permute-done.28.refs_1_), channel_id=1, source_target_pairs={{0,1},{1,0},{2,3},{3,2},{4,5},{5,4},{6,7},{7,6},{8,9},{9,8},{10,11... | collective-permute-start | bytes 1179656 | tf_op jit(solution)/shard_map/ppermute | solution.py:292
  (22 other events, 125.2 us)
